TPU v7x, 64 devices: a 2x2x8 block of a 4x4x8 slice. The times are simulated.
64 devices in a mesh: dp: 4 (over x, y), cp: 16 (over z, core).
Axes of the slice: x: 2, y: 2, z: 8, core: 2. Of those that a mesh axis runs over, the one named last changes fastest.
The devices are a block of a 4x4x8 slice.
Arguments:
- queries: bfloat16 [1536, 64, 128], P(('dp', 'cp')), parts along dimension 0
- key_new: bfloat16 [1536, 8, 128], P(('dp', 'cp')), parts along dimension 0
- value_new: bfloat16 [1536, 8, 128], P(('dp', 'cp')), parts along dimension 0
- key_cache: bfloat16 [131072, 8, 128], P(('dp', 'cp')), parts along dimension 0
- value_cache: bfloat16 [131072, 8, 128], P(('dp', 'cp')), parts along dimension 0
- prefix_len: int32 [4], P('dp'), parts along dimension 0
Outputs:
- output 1: bfloat16 [1536, 64, 128], P(('dp', 'cp')), parts along dimension 0
- output 2: float32 [1536, 64], P(('dp', 'cp')), parts along dimension 0
There are 4 independent parts. A program takes and returns all parts, laid end to end along the dimension named above; each array names one.
All inputs are finite; a program needn't handle non-finite values.
Results may differ from a plain program's by a relative error of at most 0.00914856.
Values are sent between devices in bfloat16 or wider.
A program may use at most 768 MiB of HBM per device.

v0:
```python
import jax
import jax.numpy as jnp
from jax import lax
from jax.sharding import PartitionSpec as P

MASK_FILL = -1e30


def solution(mesh):
    groups = mesh.shape['cp']
    send_pairs = [(src_idx, (src_idx + 1) % groups) for src_idx in range(groups)]
    tok_spec = P(('dp', 'cp'))

    def local_attend(queries, key_new, value_new, key_cache, value_cache, prefix_len):
        tok_rows, num_heads, head_dim = queries.shape
        cache_len, kv_heads = key_cache.shape[0], key_cache.shape[1]
        group_ratio = num_heads // kv_heads
        logit_scale = head_dim ** -0.5
        my_rank = lax.axis_index('cp')
        cache_seen = my_rank * cache_len + jnp.arange(cache_len) < prefix_len[0]
        row_ids = jnp.arange(tok_rows)
        key_ids = my_rank * tok_rows + row_ids

        def absorb(loop_step, q_blk, out_acc, row_max, row_sum):
            source = (my_rank - loop_step) % groups
            q_grouped = q_blk.reshape(tok_rows, kv_heads, group_ratio, head_dim)
            s_cache = jnp.einsum('tkgd,skd->kgts', q_grouped, key_cache, preferred_element_type=jnp.float32) * logit_scale
            s_cache = jnp.where(cache_seen, s_cache, MASK_FILL)
            s_fresh = jnp.einsum('tkgd,skd->kgts', q_grouped, key_new, preferred_element_type=jnp.float32) * logit_scale
            fresh_seen = key_ids[None, :] <= (source * tok_rows + row_ids)[:, None]
            s_fresh = jnp.where(fresh_seen, s_fresh, MASK_FILL)
            next_max = jnp.maximum(row_max, jnp.maximum(s_cache.max(axis=-1), s_fresh.max(axis=-1)))
            e_cache = jnp.exp(s_cache - next_max[..., None])
            e_fresh = jnp.exp(s_fresh - next_max[..., None])
            rescale_by = jnp.exp(row_max - next_max)
            row_sum = row_sum * rescale_by + e_cache.sum(axis=-1) + e_fresh.sum(axis=-1)
            out_acc = (out_acc * rescale_by[..., None]
                       + jnp.einsum('kgts,skd->kgtd', e_cache.astype(jnp.bfloat16), value_cache, preferred_element_type=jnp.float32)
                       + jnp.einsum('kgts,skd->kgtd', e_fresh.astype(jnp.bfloat16), value_new, preferred_element_type=jnp.float32))
            return out_acc, next_max, row_sum

        def one_step(loop_step, state):
            q_blk, out_acc, row_max, row_sum = state
            out_acc, row_max, row_sum = absorb(loop_step, q_blk, out_acc, row_max, row_sum)
            return lax.ppermute((q_blk, out_acc, row_max, row_sum), 'cp', send_pairs)

        start_acc = jnp.zeros((kv_heads, group_ratio, tok_rows, head_dim), jnp.float32)
        start_max = jnp.full((kv_heads, group_ratio, tok_rows), MASK_FILL, jnp.float32)
        start_sum = jnp.zeros((kv_heads, group_ratio, tok_rows), jnp.float32)
        q_blk, out_acc, row_max, row_sum = lax.fori_loop(0, groups - 1, one_step, (queries, start_acc, start_max, start_sum))
        out_acc, row_max, row_sum = absorb(groups - 1, q_blk, out_acc, row_max, row_sum)
        out_acc, row_max, row_sum = lax.ppermute((out_acc, row_max, row_sum), 'cp', send_pairs)
        attn_out = (out_acc / row_sum[..., None]).transpose(2, 0, 1, 3).reshape(tok_rows, num_heads, head_dim).astype(jnp.bfloat16)
        row_lse = (row_max + jnp.log(row_sum)).transpose(2, 0, 1).reshape(tok_rows, num_heads)
        return attn_out, row_lse

    return jax.shard_map(local_attend, mesh=mesh, in_specs=(tok_spec, tok_spec, tok_spec, tok_spec, tok_spec, P('dp')), out_specs=(tok_spec, tok_spec), check_vma=False)
```

profile of v0, /device:TPU:28, one launch (start us, length us, event | category | flops | bytes accessed | tf_op | source)
XLA Modules:
  0.0 608.4 jit_solution(13646896641715399051)
XLA Ops:
  13.8 556.5 %while.22 = (s32[]{:T(128)}, bf16[24,64,128]{2,0,1:T(8,128)(2,1)S(1)}, f32[8,8,24,128]{3,2,1,0:T(8,128)}, f32[8,8,24]{2,1,0:T(8,128)S(1)}, f32[8,8,24]{2,1,0:T(8...) while((s32[]{:T(128)}, ...), condition=%wide.region_5.6_spmd.clone, body=%wide.region_0.5_spmd.clone.sunk | while | flops 1664945664 | bytes 59443184 | solution.py:50
  23.4 7.2 %fusion.87 = f32[8,8,24,128]{3,2,1,0:T(8,128)} fusion(bf16[2048,8,128]{2,0,1:T(8,128)(2,1)} %get-tuple-element.586, f32[8,2048,24,8]{1,2,3,0:T(8,128)S(1)} %get-tuple-element.536, f32[8,8,24]{2,1,0:T(8,128)S(1)} %maximum_maximum_fusion.3, pred[2048]{0:T(1024)(128)(4,1)S(1)} %add_compare_fusion.3, f32[8,8,24,128]{3,2,1,0:T(8,128)} %get-tuple-element.562, ...), kind=kOutput, calls=%fused_computation.21.clone.1 | convolution fusion | flops 818282496 | bytes 18364416 | tf_op jit(solution)/shard_map/while/body/eval_jaxpr/kgts,skd->kgtd/dot_general | solution.py:38
  36.6 16.6 %collective-permute-done.2 = f32[8,8,24]{2,1,0:T(8,128)S(1)} collective-permute-done((f32[8,8,24]{2,1,0:T(8,128)S(1)}, f32[8,8,24]{2,1,0:T(8,128)S(1)}, u32[]{:S(2)}, u32[]{:S(2)}) %collective-permute-start.2) | collective-permute-done | bytes 6176 | tf_op jit(solution)/shard_map/while/body/eval_jaxpr/ppermute | solution.py:45
  64.1 7.2 %fusion.87 = f32[8,8,24,128]{3,2,1,0:T(8,128)} fusion(bf16[2048,8,128]{2,0,1:T(8,128)(2,1)} %get-tuple-element.586, f32[8,2048,24,8]{1,2,3,0:T(8,128)S(1)} %get-tuple-element.536, f32[8,8,24]{2,1,0:T(8,128)S(1)} %maximum_maximum_fusion.3, pred[2048]{0:T(1024)(128)(4,1)S(1)} %add_compare_fusion.3, f32[8,8,24,128]{3,2,1,0:T(8,128)} %get-tuple-element.562, ...), kind=kOutput, calls=%fused_computation.21.clone.1 | convolution fusion | flops 818282496 | bytes 18364416 | tf_op jit(solution)/shard_map/while/body/eval_jaxpr/kgts,skd->kgtd/dot_general | solution.py:38
  73.1 16.9 %collective-permute-done.2 = f32[8,8,24]{2,1,0:T(8,128)S(1)} collective-permute-done((f32[8,8,24]{2,1,0:T(8,128)S(1)}, f32[8,8,24]{2,1,0:T(8,128)S(1)}, u32[]{:S(2)}, u32[]{:S(2)}) %collective-permute-start.2) | collective-permute-done | bytes 6176 | tf_op jit(solution)/shard_map/while/body/eval_jaxpr/ppermute | solution.py:45
  100.9 7.2 %fusion.87 = f32[8,8,24,128]{3,2,1,0:T(8,128)} fusion(bf16[2048,8,128]{2,0,1:T(8,128)(2,1)} %get-tuple-element.586, f32[8,2048,24,8]{1,2,3,0:T(8,128)S(1)} %get-tuple-element.536, f32[8,8,24]{2,1,0:T(8,128)S(1)} %maximum_maximum_fusion.3, pred[2048]{0:T(1024)(128)(4,1)S(1)} %add_compare_fusion.3, f32[8,8,24,128]{3,2,1,0:T(8,128)} %get-tuple-element.562, ...), kind=kOutput, calls=%fused_computation.21.clone.1 | convolution fusion | flops 818282496 | bytes 18364416 | tf_op jit(solution)/shard_map/while/body/eval_jaxpr/kgts,skd->kgtd/dot_general | solution.py:38
  109.9 16.9 %collective-permute-done.2 = f32[8,8,24]{2,1,0:T(8,128)S(1)} collective-permute-done((f32[8,8,24]{2,1,0:T(8,128)S(1)}, f32[8,8,24]{2,1,0:T(8,128)S(1)}, u32[]{:S(2)}, u32[]{:S(2)}) %collective-permute-start.2) | collective-permute-done | bytes 6176 | tf_op jit(solution)/shard_map/while/body/eval_jaxpr/ppermute | solution.py:45
  137.8 7.2 %fusion.87 = f32[8,8,24,128]{3,2,1,0:T(8,128)} fusion(bf16[2048,8,128]{2,0,1:T(8,128)(2,1)} %get-tuple-element.586, f32[8,2048,24,8]{1,2,3,0:T(8,128)S(1)} %get-tuple-element.536, f32[8,8,24]{2,1,0:T(8,128)S(1)} %maximum_maximum_fusion.3, pred[2048]{0:T(1024)(128)(4,1)S(1)} %add_compare_fusion.3, f32[8,8,24,128]{3,2,1,0:T(8,128)} %get-tuple-element.562, ...), kind=kOutput, calls=%fused_computation.21.clone.1 | convolution fusion | flops 818282496 | bytes 18364416 | tf_op jit(solution)/shard_map/while/body/eval_jaxpr/kgts,skd->kgtd/dot_general | solution.py:38
  146.7 16.9 %collective-permute-done.2 = f32[8,8,24]{2,1,0:T(8,128)S(1)} collective-permute-done((f32[8,8,24]{2,1,0:T(8,128)S(1)}, f32[8,8,24]{2,1,0:T(8,128)S(1)}, u32[]{:S(2)}, u32[]{:S(2)}) %collective-permute-start.2) | collective-permute-done | bytes 6176 | tf_op jit(solution)/shard_map/while/body/eval_jaxpr/ppermute | solution.py:45
  174.6 7.2 %fusion.87 = f32[8,8,24,128]{3,2,1,0:T(8,128)} fusion(bf16[2048,8,128]{2,0,1:T(8,128)(2,1)} %get-tuple-element.586, f32[8,2048,24,8]{1,2,3,0:T(8,128)S(1)} %get-tuple-element.536, f32[8,8,24]{2,1,0:T(8,128)S(1)} %maximum_maximum_fusion.3, pred[2048]{0:T(1024)(128)(4,1)S(1)} %add_compare_fusion.3, f32[8,8,24,128]{3,2,1,0:T(8,128)} %get-tuple-element.562, ...), kind=kOutput, calls=%fused_computation.21.clone.1 | convolution fusion | flops 818282496 | bytes 18364416 | tf_op jit(solution)/shard_map/while/body/eval_jaxpr/kgts,skd->kgtd/dot_general | solution.py:38
  183.6 16.9 %collective-permute-done.2 = f32[8,8,24]{2,1,0:T(8,128)S(1)} collective-permute-done((f32[8,8,24]{2,1,0:T(8,128)S(1)}, f32[8,8,24]{2,1,0:T(8,128)S(1)}, u32[]{:S(2)}, u32[]{:S(2)}) %collective-permute-start.2) | collective-permute-done | bytes 6176 | tf_op jit(solution)/shard_map/while/body/eval_jaxpr/ppermute | solution.py:45
  211.5 7.2 %fusion.87 = f32[8,8,24,128]{3,2,1,0:T(8,128)} fusion(bf16[2048,8,128]{2,0,1:T(8,128)(2,1)} %get-tuple-element.586, f32[8,2048,24,8]{1,2,3,0:T(8,128)S(1)} %get-tuple-element.536, f32[8,8,24]{2,1,0:T(8,128)S(1)} %maximum_maximum_fusion.3, pred[2048]{0:T(1024)(128)(4,1)S(1)} %add_compare_fusion.3, f32[8,8,24,128]{3,2,1,0:T(8,128)} %get-tuple-element.562, ...), kind=kOutput, calls=%fused_computation.21.clone.1 | convolution fusion | flops 818282496 | bytes 18364416 | tf_op jit(solution)/shard_map/while/body/eval_jaxpr/kgts,skd->kgtd/dot_general | solution.py:38
  220.4 16.9 %collective-permute-done.2 = f32[8,8,24]{2,1,0:T(8,128)S(1)} collective-permute-done((f32[8,8,24]{2,1,0:T(8,128)S(1)}, f32[8,8,24]{2,1,0:T(8,128)S(1)}, u32[]{:S(2)}, u32[]{:S(2)}) %collective-permute-start.2) | collective-permute-done | bytes 6176 | tf_op jit(solution)/shard_map/while/body/eval_jaxpr/ppermute | solution.py:45
  248.3 7.2 %fusion.87 = f32[8,8,24,128]{3,2,1,0:T(8,128)} fusion(bf16[2048,8,128]{2,0,1:T(8,128)(2,1)} %get-tuple-element.586, f32[8,2048,24,8]{1,2,3,0:T(8,128)S(1)} %get-tuple-element.536, f32[8,8,24]{2,1,0:T(8,128)S(1)} %maximum_maximum_fusion.3, pred[2048]{0:T(1024)(128)(4,1)S(1)} %add_compare_fusion.3, f32[8,8,24,128]{3,2,1,0:T(8,128)} %get-tuple-element.562, ...), kind=kOutput, calls=%fused_computation.21.clone.1 | convolution fusion | flops 818282496 | bytes 18364416 | tf_op jit(solution)/shard_map/while/body/eval_jaxpr/kgts,skd->kgtd/dot_general | solution.py:38
  257.3 16.9 %collective-permute-done.2 = f32[8,8,24]{2,1,0:T(8,128)S(1)} collective-permute-done((f32[8,8,24]{2,1,0:T(8,128)S(1)}, f32[8,8,24]{2,1,0:T(8,128)S(1)}, u32[]{:S(2)}, u32[]{:S(2)}) %collective-permute-start.2) | collective-permute-done | bytes 6176 | tf_op jit(solution)/shard_map/while/body/eval_jaxpr/ppermute | solution.py:45
  285.1 7.2 %fusion.87 = f32[8,8,24,128]{3,2,1,0:T(8,128)} fusion(bf16[2048,8,128]{2,0,1:T(8,128)(2,1)} %get-tuple-element.586, f32[8,2048,24,8]{1,2,3,0:T(8,128)S(1)} %get-tuple-element.536, f32[8,8,24]{2,1,0:T(8,128)S(1)} %maximum_maximum_fusion.3, pred[2048]{0:T(1024)(128)(4,1)S(1)} %add_compare_fusion.3, f32[8,8,24,128]{3,2,1,0:T(8,128)} %get-tuple-element.562, ...), kind=kOutput, calls=%fused_computation.21.clone.1 | convolution fusion | flops 818282496 | bytes 18364416 | tf_op jit(solution)/shard_map/while/body/eval_jaxpr/kgts,skd->kgtd/dot_general | solution.py:38
  294.1 16.9 %collective-permute-done.2 = f32[8,8,24]{2,1,0:T(8,128)S(1)} collective-permute-done((f32[8,8,24]{2,1,0:T(8,128)S(1)}, f32[8,8,24]{2,1,0:T(8,128)S(1)}, u32[]{:S(2)}, u32[]{:S(2)}) %collective-permute-start.2) | collective-permute-done | bytes 6176 | tf_op jit(solution)/shard_map/while/body/eval_jaxpr/ppermute | solution.py:45
  322.0 7.2 %fusion.87 = f32[8,8,24,128]{3,2,1,0:T(8,128)} fusion(bf16[2048,8,128]{2,0,1:T(8,128)(2,1)} %get-tuple-element.586, f32[8,2048,24,8]{1,2,3,0:T(8,128)S(1)} %get-tuple-element.536, f32[8,8,24]{2,1,0:T(8,128)S(1)} %maximum_maximum_fusion.3, pred[2048]{0:T(1024)(128)(4,1)S(1)} %add_compare_fusion.3, f32[8,8,24,128]{3,2,1,0:T(8,128)} %get-tuple-element.562, ...), kind=kOutput, calls=%fused_computation.21.clone.1 | convolution fusion | flops 818282496 | bytes 18364416 | tf_op jit(solution)/shard_map/while/body/eval_jaxpr/kgts,skd->kgtd/dot_general | solution.py:38
  331.0 16.9 %collective-permute-done.2 = f32[8,8,24]{2,1,0:T(8,128)S(1)} collective-permute-done((f32[8,8,24]{2,1,0:T(8,128)S(1)}, f32[8,8,24]{2,1,0:T(8,128)S(1)}, u32[]{:S(2)}, u32[]{:S(2)}) %collective-permute-start.2) | collective-permute-done | bytes 6176 | tf_op jit(solution)/shard_map/while/body/eval_jaxpr/ppermute | solution.py:45
  358.8 7.2 %fusion.87 = f32[8,8,24,128]{3,2,1,0:T(8,128)} fusion(bf16[2048,8,128]{2,0,1:T(8,128)(2,1)} %get-tuple-element.586, f32[8,2048,24,8]{1,2,3,0:T(8,128)S(1)} %get-tuple-element.536, f32[8,8,24]{2,1,0:T(8,128)S(1)} %maximum_maximum_fusion.3, pred[2048]{0:T(1024)(128)(4,1)S(1)} %add_compare_fusion.3, f32[8,8,24,128]{3,2,1,0:T(8,128)} %get-tuple-element.562, ...), kind=kOutput, calls=%fused_computation.21.clone.1 | convolution fusion | flops 818282496 | bytes 18364416 | tf_op jit(solution)/shard_map/while/body/eval_jaxpr/kgts,skd->kgtd/dot_general | solution.py:38
  367.8 16.9 %collective-permute-done.2 = f32[8,8,24]{2,1,0:T(8,128)S(1)} collective-permute-done((f32[8,8,24]{2,1,0:T(8,128)S(1)}, f32[8,8,24]{2,1,0:T(8,128)S(1)}, u32[]{:S(2)}, u32[]{:S(2)}) %collective-permute-start.2) | collective-permute-done | bytes 6176 | tf_op jit(solution)/shard_map/while/body/eval_jaxpr/ppermute | solution.py:45
  395.7 7.2 %fusion.87 = f32[8,8,24,128]{3,2,1,0:T(8,128)} fusion(bf16[2048,8,128]{2,0,1:T(8,128)(2,1)} %get-tuple-element.586, f32[8,2048,24,8]{1,2,3,0:T(8,128)S(1)} %get-tuple-element.536, f32[8,8,24]{2,1,0:T(8,128)S(1)} %maximum_maximum_fusion.3, pred[2048]{0:T(1024)(128)(4,1)S(1)} %add_compare_fusion.3, f32[8,8,24,128]{3,2,1,0:T(8,128)} %get-tuple-element.562, ...), kind=kOutput, calls=%fused_computation.21.clone.1 | convolution fusion | flops 818282496 | bytes 18364416 | tf_op jit(solution)/shard_map/while/body/eval_jaxpr/kgts,skd->kgtd/dot_general | solution.py:38
  404.6 16.9 %collective-permute-done.2 = f32[8,8,24]{2,1,0:T(8,128)S(1)} collective-permute-done((f32[8,8,24]{2,1,0:T(8,128)S(1)}, f32[8,8,24]{2,1,0:T(8,128)S(1)}, u32[]{:S(2)}, u32[]{:S(2)}) %collective-permute-start.2) | collective-permute-done | bytes 6176 | tf_op jit(solution)/shard_map/while/body/eval_jaxpr/ppermute | solution.py:45
  432.5 7.2 %fusion.87 = f32[8,8,24,128]{3,2,1,0:T(8,128)} fusion(bf16[2048,8,128]{2,0,1:T(8,128)(2,1)} %get-tuple-element.586, f32[8,2048,24,8]{1,2,3,0:T(8,128)S(1)} %get-tuple-element.536, f32[8,8,24]{2,1,0:T(8,128)S(1)} %maximum_maximum_fusion.3, pred[2048]{0:T(1024)(128)(4,1)S(1)} %add_compare_fusion.3, f32[8,8,24,128]{3,2,1,0:T(8,128)} %get-tuple-element.562, ...), kind=kOutput, calls=%fused_computation.21.clone.1 | convolution fusion | flops 818282496 | bytes 18364416 | tf_op jit(solution)/shard_map/while/body/eval_jaxpr/kgts,skd->kgtd/dot_general | solution.py:38
  441.5 16.9 %collective-permute-done.2 = f32[8,8,24]{2,1,0:T(8,128)S(1)} collective-permute-done((f32[8,8,24]{2,1,0:T(8,128)S(1)}, f32[8,8,24]{2,1,0:T(8,128)S(1)}, u32[]{:S(2)}, u32[]{:S(2)}) %collective-permute-start.2) | collective-permute-done | bytes 6176 | tf_op jit(solution)/shard_map/while/body/eval_jaxpr/ppermute | solution.py:45
  469.4 7.2 %fusion.87 = f32[8,8,24,128]{3,2,1,0:T(8,128)} fusion(bf16[2048,8,128]{2,0,1:T(8,128)(2,1)} %get-tuple-element.586, f32[8,2048,24,8]{1,2,3,0:T(8,128)S(1)} %get-tuple-element.536, f32[8,8,24]{2,1,0:T(8,128)S(1)} %maximum_maximum_fusion.3, pred[2048]{0:T(1024)(128)(4,1)S(1)} %add_compare_fusion.3, f32[8,8,24,128]{3,2,1,0:T(8,128)} %get-tuple-element.562, ...), kind=kOutput, calls=%fused_computation.21.clone.1 | convolution fusion | flops 818282496 | bytes 18364416 | tf_op jit(solution)/shard_map/while/body/eval_jaxpr/kgts,skd->kgtd/dot_general | solution.py:38
  478.3 16.9 %collective-permute-done.2 = f32[8,8,24]{2,1,0:T(8,128)S(1)} collective-permute-done((f32[8,8,24]{2,1,0:T(8,128)S(1)}, f32[8,8,24]{2,1,0:T(8,128)S(1)}, u32[]{:S(2)}, u32[]{:S(2)}) %collective-permute-start.2) | collective-permute-done | bytes 6176 | tf_op jit(solution)/shard_map/while/body/eval_jaxpr/ppermute | solution.py:45
  515.2 16.9 %collective-permute-done.2 = f32[8,8,24]{2,1,0:T(8,128)S(1)} collective-permute-done((f32[8,8,24]{2,1,0:T(8,128)S(1)}, f32[8,8,24]{2,1,0:T(8,128)S(1)}, u32[]{:S(2)}, u32[]{:S(2)}) %collective-permute-start.2) | collective-permute-done | bytes 6176 | tf_op jit(solution)/shard_map/while/body/eval_jaxpr/ppermute | solution.py:45
  543.0 7.2 %fusion.87 = f32[8,8,24,128]{3,2,1,0:T(8,128)} fusion(bf16[2048,8,128]{2,0,1:T(8,128)(2,1)} %get-tuple-element.586, f32[8,2048,24,8]{1,2,3,0:T(8,128)S(1)} %get-tuple-element.536, f32[8,8,24]{2,1,0:T(8,128)S(1)} %maximum_maximum_fusion.3, pred[2048]{0:T(1024)(128)(4,1)S(1)} %add_compare_fusion.3, f32[8,8,24,128]{3,2,1,0:T(8,128)} %get-tuple-element.562, ...), kind=kOutput, calls=%fused_computation.21.clone.1 | convolution fusion | flops 818282496 | bytes 18364416 | tf_op jit(solution)/shard_map/while/body/eval_jaxpr/kgts,skd->kgtd/dot_general | solution.py:38
  552.0 16.9 %collective-permute-done.2 = f32[8,8,24]{2,1,0:T(8,128)S(1)} collective-permute-done((f32[8,8,24]{2,1,0:T(8,128)S(1)}, f32[8,8,24]{2,1,0:T(8,128)S(1)}, u32[]{:S(2)}, u32[]{:S(2)}) %collective-permute-start.2) | collective-permute-done | bytes 6176 | tf_op jit(solution)/shard_map/while/body/eval_jaxpr/ppermute | solution.py:45
  583.1 8.3 %fusion.47 = f32[8,8,24,128]{3,1,2,0:T(8,128)S(1)} fusion(bf16[2048,8,128,1]{2,1,0,3:T(8,128)(2,1)} %bitcast.99, f32[8,24,8,2048]{3,2,1,0:T(8,128)} %copy-done, f32[8,8,24]{1,2,0:T(8,128)S(1)} %maximum_maximum_fusion.1, pred[2048]{0:T(1024)(128)(4,1)S(1)} %add_compare_fusion.1, f32[8,8,24,128]{3,2,1,0:T(8,128)S(1)} %copy-done.2, ...), kind=kOutput, calls=%fused_computation.55 | convolution fusion | flops 818282496 | bytes 18364416 | tf_op jit(solution)/shard_map/kgts,skd->kgtd/dot_general | solution.py:38
  592.0 13.5 %collective-permute-done.5 = f32[8,8,24]{1,2,0:T(8,128)S(1)} collective-permute-done((f32[8,8,24]{1,2,0:T(8,128)S(1)}, f32[8,8,24]{1,2,0:T(8,128)S(1)}, u32[]{:S(2)}, u32[]{:S(2)}) %collective-permute-start.5) | collective-permute-done | bytes 6176 | tf_op jit(solution)/shard_map/ppermute | solution.py:52
  (353 shorter events, 228.8 us)
Async XLA Ops:
  32.1 21.4 %collective-permute-start.1 = (f32[8,8,24,128]{3,2,1,0:T(8,128)S(1)}, f32[8,8,24,128]{3,2,1,0:T(8,128)S(1)}, u32[]{:S(2)}, u32[]{:S(2)}) collective-permute-start(f32[8,8,24,128]{3,2,1,0:T(8,128)S(1)} %convolution_add_fusion.3), channel_id=1, source_target_pairs={{0,1},{1,2},{2,3},{3,4},{4,5},{5,6},{6,7},{7,8},{8,9},{9,10},{10,1... | collective-permute-start | bytes 2359304 | tf_op jit(solution)/shard_map/while/body/eval_jaxpr/ppermute | solution.py:45
  32.1 21.4 %collective-permute-start = (bf16[24,64,128]{2,0,1:T(8,128)(2,1)S(1)}, bf16[24,64,128]{2,0,1:T(8,128)(2,1)S(1)}, u32[]{:S(2)}, u32[]{:S(2)}) collective-permute-start(bf16[24,64,128]{2,0,1:T(8,128)(2,1)S(1)} %copy.136), channel_id=1, source_target_pairs={{0,1},{1,2},{2,3},{3,4},{4,5},{5,6},{6,7},{7,8},{8,9},{9,10},{10,1... | collective-permute-start | bytes 1179656 | tf_op jit(solution)/shard_map/while/body/eval_jaxpr/ppermute | solution.py:45
  34.4 18.8 %collective-permute-start.2 = (f32[8,8,24]{2,1,0:T(8,128)S(1)}, f32[8,8,24]{2,1,0:T(8,128)S(1)}, u32[]{:S(2)}, u32[]{:S(2)}) collective-permute-start(f32[8,8,24]{2,1,0:T(8,128)S(1)} %maximum_maximum_fusion.3), channel_id=1, source_target_pairs={{0,1},{1,2},{2,3},{3,4},{4,5},{5,6},{6,7},{7,8},{8,9},{9,10},{10,1... | collective-permute-start | bytes 18440 | tf_op jit(solution)/shard_map/while/body/eval_jaxpr/ppermute | solution.py:45
  34.4 19.1 %collective-permute-start.3 = (f32[8,8,24]{2,1,0:T(8,128)S(1)}, f32[8,8,24]{2,1,0:T(8,128)S(1)}, u32[]{:S(2)}, u32[]{:S(2)}) collective-permute-start(f32[8,8,24]{2,1,0:T(8,128)S(1)} %get-tuple-element.541), channel_id=1, source_target_pairs={{0,1},{1,2},{2,3},{3,4},{4,5},{5,6},{6,7},{7,8},{8,9},{9,10},{10,1... | collective-permute-start | bytes 18440 | tf_op jit(solution)/shard_map/while/body/eval_jaxpr/ppermute | solution.py:45
  72.8 17.6 %collective-permute-start.1 = (f32[8,8,24,128]{3,2,1,0:T(8,128)S(1)}, f32[8,8,24,128]{3,2,1,0:T(8,128)S(1)}, u32[]{:S(2)}, u32[]{:S(2)}) collective-permute-start(f32[8,8,24,128]{3,2,1,0:T(8,128)S(1)} %convolution_add_fusion.3), channel_id=1, source_target_pairs={{0,1},{1,2},{2,3},{3,4},{4,5},{5,6},{6,7},{7,8},{8,9},{9,10},{10,1... | collective-permute-start | bytes 2359304 | tf_op jit(solution)/shard_map/while/body/eval_jaxpr/ppermute | solution.py:45
  72.8 17.5 %collective-permute-start = (bf16[24,64,128]{2,0,1:T(8,128)(2,1)S(1)}, bf16[24,64,128]{2,0,1:T(8,128)(2,1)S(1)}, u32[]{:S(2)}, u32[]{:S(2)}) collective-permute-start(bf16[24,64,128]{2,0,1:T(8,128)(2,1)S(1)} %copy.136), channel_id=1, source_target_pairs={{0,1},{1,2},{2,3},{3,4},{4,5},{5,6},{6,7},{7,8},{8,9},{9,10},{10,1... | collective-permute-start | bytes 1179656 | tf_op jit(solution)/shard_map/while/body/eval_jaxpr/ppermute | solution.py:45
  109.6 17.6 %collective-permute-start.1 = (f32[8,8,24,128]{3,2,1,0:T(8,128)S(1)}, f32[8,8,24,128]{3,2,1,0:T(8,128)S(1)}, u32[]{:S(2)}, u32[]{:S(2)}) collective-permute-start(f32[8,8,24,128]{3,2,1,0:T(8,128)S(1)} %convolution_add_fusion.3), channel_id=1, source_target_pairs={{0,1},{1,2},{2,3},{3,4},{4,5},{5,6},{6,7},{7,8},{8,9},{9,10},{10,1... | collective-permute-start | bytes 2359304 | tf_op jit(solution)/shard_map/while/body/eval_jaxpr/ppermute | solution.py:45
  109.7 17.5 %collective-permute-start = (bf16[24,64,128]{2,0,1:T(8,128)(2,1)S(1)}, bf16[24,64,128]{2,0,1:T(8,128)(2,1)S(1)}, u32[]{:S(2)}, u32[]{:S(2)}) collective-permute-start(bf16[24,64,128]{2,0,1:T(8,128)(2,1)S(1)} %copy.136), channel_id=1, source_target_pairs={{0,1},{1,2},{2,3},{3,4},{4,5},{5,6},{6,7},{7,8},{8,9},{9,10},{10,1... | collective-permute-start | bytes 1179656 | tf_op jit(solution)/shard_map/while/body/eval_jaxpr/ppermute | solution.py:45
  146.4 17.6 %collective-permute-start.1 = (f32[8,8,24,128]{3,2,1,0:T(8,128)S(1)}, f32[8,8,24,128]{3,2,1,0:T(8,128)S(1)}, u32[]{:S(2)}, u32[]{:S(2)}) collective-permute-start(f32[8,8,24,128]{3,2,1,0:T(8,128)S(1)} %convolution_add_fusion.3), channel_id=1, source_target_pairs={{0,1},{1,2},{2,3},{3,4},{4,5},{5,6},{6,7},{7,8},{8,9},{9,10},{10,1... | collective-permute-start | bytes 2359304 | tf_op jit(solution)/shard_map/while/body/eval_jaxpr/ppermute | solution.py:45
  146.5 17.5 %collective-permute-start = (bf16[24,64,128]{2,0,1:T(8,128)(2,1)S(1)}, bf16[24,64,128]{2,0,1:T(8,128)(2,1)S(1)}, u32[]{:S(2)}, u32[]{:S(2)}) collective-permute-start(bf16[24,64,128]{2,0,1:T(8,128)(2,1)S(1)} %copy.136), channel_id=1, source_target_pairs={{0,1},{1,2},{2,3},{3,4},{4,5},{5,6},{6,7},{7,8},{8,9},{9,10},{10,1... | collective-permute-start | bytes 1179656 | tf_op jit(solution)/shard_map/while/body/eval_jaxpr/ppermute | solution.py:45
  183.3 17.6 %collective-permute-start.1 = (f32[8,8,24,128]{3,2,1,0:T(8,128)S(1)}, f32[8,8,24,128]{3,2,1,0:T(8,128)S(1)}, u32[]{:S(2)}, u32[]{:S(2)}) collective-permute-start(f32[8,8,24,128]{3,2,1,0:T(8,128)S(1)} %convolution_add_fusion.3), channel_id=1, source_target_pairs={{0,1},{1,2},{2,3},{3,4},{4,5},{5,6},{6,7},{7,8},{8,9},{9,10},{10,1... | collective-permute-start | bytes 2359304 | tf_op jit(solution)/shard_map/while/body/eval_jaxpr/ppermute | solution.py:45
  183.4 17.5 %collective-permute-start = (bf16[24,64,128]{2,0,1:T(8,128)(2,1)S(1)}, bf16[24,64,128]{2,0,1:T(8,128)(2,1)S(1)}, u32[]{:S(2)}, u32[]{:S(2)}) collective-permute-start(bf16[24,64,128]{2,0,1:T(8,128)(2,1)S(1)} %copy.136), channel_id=1, source_target_pairs={{0,1},{1,2},{2,3},{3,4},{4,5},{5,6},{6,7},{7,8},{8,9},{9,10},{10,1... | collective-permute-start | bytes 1179656 | tf_op jit(solution)/shard_map/while/body/eval_jaxpr/ppermute | solution.py:45
  220.1 17.6 %collective-permute-start.1 = (f32[8,8,24,128]{3,2,1,0:T(8,128)S(1)}, f32[8,8,24,128]{3,2,1,0:T(8,128)S(1)}, u32[]{:S(2)}, u32[]{:S(2)}) collective-permute-start(f32[8,8,24,128]{3,2,1,0:T(8,128)S(1)} %convolution_add_fusion.3), channel_id=1, source_target_pairs={{0,1},{1,2},{2,3},{3,4},{4,5},{5,6},{6,7},{7,8},{8,9},{9,10},{10,1... | collective-permute-start | bytes 2359304 | tf_op jit(solution)/shard_map/while/body/eval_jaxpr/ppermute | solution.py:45
  220.2 17.5 %collective-permute-start = (bf16[24,64,128]{2,0,1:T(8,128)(2,1)S(1)}, bf16[24,64,128]{2,0,1:T(8,128)(2,1)S(1)}, u32[]{:S(2)}, u32[]{:S(2)}) collective-permute-start(bf16[24,64,128]{2,0,1:T(8,128)(2,1)S(1)} %copy.136), channel_id=1, source_target_pairs={{0,1},{1,2},{2,3},{3,4},{4,5},{5,6},{6,7},{7,8},{8,9},{9,10},{10,1... | collective-permute-start | bytes 1179656 | tf_op jit(solution)/shard_map/while/body/eval_jaxpr/ppermute | solution.py:45
  257.0 17.6 %collective-permute-start.1 = (f32[8,8,24,128]{3,2,1,0:T(8,128)S(1)}, f32[8,8,24,128]{3,2,1,0:T(8,128)S(1)}, u32[]{:S(2)}, u32[]{:S(2)}) collective-permute-start(f32[8,8,24,128]{3,2,1,0:T(8,128)S(1)} %convolution_add_fusion.3), channel_id=1, source_target_pairs={{0,1},{1,2},{2,3},{3,4},{4,5},{5,6},{6,7},{7,8},{8,9},{9,10},{10,1... | collective-permute-start | bytes 2359304 | tf_op jit(solution)/shard_map/while/body/eval_jaxpr/ppermute | solution.py:45
  257.0 17.5 %collective-permute-start = (bf16[24,64,128]{2,0,1:T(8,128)(2,1)S(1)}, bf16[24,64,128]{2,0,1:T(8,128)(2,1)S(1)}, u32[]{:S(2)}, u32[]{:S(2)}) collective-permute-start(bf16[24,64,128]{2,0,1:T(8,128)(2,1)S(1)} %copy.136), channel_id=1, source_target_pairs={{0,1},{1,2},{2,3},{3,4},{4,5},{5,6},{6,7},{7,8},{8,9},{9,10},{10,1... | collective-permute-start | bytes 1179656 | tf_op jit(solution)/shard_map/while/body/eval_jaxpr/ppermute | solution.py:45
  293.8 17.6 %collective-permute-start.1 = (f32[8,8,24,128]{3,2,1,0:T(8,128)S(1)}, f32[8,8,24,128]{3,2,1,0:T(8,128)S(1)}, u32[]{:S(2)}, u32[]{:S(2)}) collective-permute-start(f32[8,8,24,128]{3,2,1,0:T(8,128)S(1)} %convolution_add_fusion.3), channel_id=1, source_target_pairs={{0,1},{1,2},{2,3},{3,4},{4,5},{5,6},{6,7},{7,8},{8,9},{9,10},{10,1... | collective-permute-start | bytes 2359304 | tf_op jit(solution)/shard_map/while/body/eval_jaxpr/ppermute | solution.py:45
  293.9 17.5 %collective-permute-start = (bf16[24,64,128]{2,0,1:T(8,128)(2,1)S(1)}, bf16[24,64,128]{2,0,1:T(8,128)(2,1)S(1)}, u32[]{:S(2)}, u32[]{:S(2)}) collective-permute-start(bf16[24,64,128]{2,0,1:T(8,128)(2,1)S(1)} %copy.136), channel_id=1, source_target_pairs={{0,1},{1,2},{2,3},{3,4},{4,5},{5,6},{6,7},{7,8},{8,9},{9,10},{10,1... | collective-permute-start | bytes 1179656 | tf_op jit(solution)/shard_map/while/body/eval_jaxpr/ppermute | solution.py:45
  330.7 17.6 %collective-permute-start.1 = (f32[8,8,24,128]{3,2,1,0:T(8,128)S(1)}, f32[8,8,24,128]{3,2,1,0:T(8,128)S(1)}, u32[]{:S(2)}, u32[]{:S(2)}) collective-permute-start(f32[8,8,24,128]{3,2,1,0:T(8,128)S(1)} %convolution_add_fusion.3), channel_id=1, source_target_pairs={{0,1},{1,2},{2,3},{3,4},{4,5},{5,6},{6,7},{7,8},{8,9},{9,10},{10,1... | collective-permute-start | bytes 2359304 | tf_op jit(solution)/shard_map/while/body/eval_jaxpr/ppermute | solution.py:45
  330.7 17.5 %collective-permute-start = (bf16[24,64,128]{2,0,1:T(8,128)(2,1)S(1)}, bf16[24,64,128]{2,0,1:T(8,128)(2,1)S(1)}, u32[]{:S(2)}, u32[]{:S(2)}) collective-permute-start(bf16[24,64,128]{2,0,1:T(8,128)(2,1)S(1)} %copy.136), channel_id=1, source_target_pairs={{0,1},{1,2},{2,3},{3,4},{4,5},{5,6},{6,7},{7,8},{8,9},{9,10},{10,1... | collective-permute-start | bytes 1179656 | tf_op jit(solution)/shard_map/while/body/eval_jaxpr/ppermute | solution.py:45
  367.5 17.6 %collective-permute-start.1 = (f32[8,8,24,128]{3,2,1,0:T(8,128)S(1)}, f32[8,8,24,128]{3,2,1,0:T(8,128)S(1)}, u32[]{:S(2)}, u32[]{:S(2)}) collective-permute-start(f32[8,8,24,128]{3,2,1,0:T(8,128)S(1)} %convolution_add_fusion.3), channel_id=1, source_target_pairs={{0,1},{1,2},{2,3},{3,4},{4,5},{5,6},{6,7},{7,8},{8,9},{9,10},{10,1... | collective-permute-start | bytes 2359304 | tf_op jit(solution)/shard_map/while/body/eval_jaxpr/ppermute | solution.py:45
  367.6 17.5 %collective-permute-start = (bf16[24,64,128]{2,0,1:T(8,128)(2,1)S(1)}, bf16[24,64,128]{2,0,1:T(8,128)(2,1)S(1)}, u32[]{:S(2)}, u32[]{:S(2)}) collective-permute-start(bf16[24,64,128]{2,0,1:T(8,128)(2,1)S(1)} %copy.136), channel_id=1, source_target_pairs={{0,1},{1,2},{2,3},{3,4},{4,5},{5,6},{6,7},{7,8},{8,9},{9,10},{10,1... | collective-permute-start | bytes 1179656 | tf_op jit(solution)/shard_map/while/body/eval_jaxpr/ppermute | solution.py:45
  404.3 17.6 %collective-permute-start.1 = (f32[8,8,24,128]{3,2,1,0:T(8,128)S(1)}, f32[8,8,24,128]{3,2,1,0:T(8,128)S(1)}, u32[]{:S(2)}, u32[]{:S(2)}) collective-permute-start(f32[8,8,24,128]{3,2,1,0:T(8,128)S(1)} %convolution_add_fusion.3), channel_id=1, source_target_pairs={{0,1},{1,2},{2,3},{3,4},{4,5},{5,6},{6,7},{7,8},{8,9},{9,10},{10,1... | collective-permute-start | bytes 2359304 | tf_op jit(solution)/shard_map/while/body/eval_jaxpr/ppermute | solution.py:45
  404.4 17.5 %collective-permute-start = (bf16[24,64,128]{2,0,1:T(8,128)(2,1)S(1)}, bf16[24,64,128]{2,0,1:T(8,128)(2,1)S(1)}, u32[]{:S(2)}, u32[]{:S(2)}) collective-permute-start(bf16[24,64,128]{2,0,1:T(8,128)(2,1)S(1)} %copy.136), channel_id=1, source_target_pairs={{0,1},{1,2},{2,3},{3,4},{4,5},{5,6},{6,7},{7,8},{8,9},{9,10},{10,1... | collective-permute-start | bytes 1179656 | tf_op jit(solution)/shard_map/while/body/eval_jaxpr/ppermute | solution.py:45
  441.2 17.6 %collective-permute-start.1 = (f32[8,8,24,128]{3,2,1,0:T(8,128)S(1)}, f32[8,8,24,128]{3,2,1,0:T(8,128)S(1)}, u32[]{:S(2)}, u32[]{:S(2)}) collective-permute-start(f32[8,8,24,128]{3,2,1,0:T(8,128)S(1)} %convolution_add_fusion.3), channel_id=1, source_target_pairs={{0,1},{1,2},{2,3},{3,4},{4,5},{5,6},{6,7},{7,8},{8,9},{9,10},{10,1... | collective-permute-start | bytes 2359304 | tf_op jit(solution)/shard_map/while/body/eval_jaxpr/ppermute | solution.py:45
  441.3 17.5 %collective-permute-start = (bf16[24,64,128]{2,0,1:T(8,128)(2,1)S(1)}, bf16[24,64,128]{2,0,1:T(8,128)(2,1)S(1)}, u32[]{:S(2)}, u32[]{:S(2)}) collective-permute-start(bf16[24,64,128]{2,0,1:T(8,128)(2,1)S(1)} %copy.136), channel_id=1, source_target_pairs={{0,1},{1,2},{2,3},{3,4},{4,5},{5,6},{6,7},{7,8},{8,9},{9,10},{10,1... | collective-permute-start | bytes 1179656 | tf_op jit(solution)/shard_map/while/body/eval_jaxpr/ppermute | solution.py:45
  478.0 17.6 %collective-permute-start.1 = (f32[8,8,24,128]{3,2,1,0:T(8,128)S(1)}, f32[8,8,24,128]{3,2,1,0:T(8,128)S(1)}, u32[]{:S(2)}, u32[]{:S(2)}) collective-permute-start(f32[8,8,24,128]{3,2,1,0:T(8,128)S(1)} %convolution_add_fusion.3), channel_id=1, source_target_pairs={{0,1},{1,2},{2,3},{3,4},{4,5},{5,6},{6,7},{7,8},{8,9},{9,10},{10,1... | collective-permute-start | bytes 2359304 | tf_op jit(solution)/shard_map/while/body/eval_jaxpr/ppermute | solution.py:45
  478.1 17.5 %collective-permute-start = (bf16[24,64,128]{2,0,1:T(8,128)(2,1)S(1)}, bf16[24,64,128]{2,0,1:T(8,128)(2,1)S(1)}, u32[]{:S(2)}, u32[]{:S(2)}) collective-permute-start(bf16[24,64,128]{2,0,1:T(8,128)(2,1)S(1)} %copy.136), channel_id=1, source_target_pairs={{0,1},{1,2},{2,3},{3,4},{4,5},{5,6},{6,7},{7,8},{8,9},{9,10},{10,1... | collective-permute-start | bytes 1179656 | tf_op jit(solution)/shard_map/while/body/eval_jaxpr/ppermute | solution.py:45
  514.9 17.6 %collective-permute-start.1 = (f32[8,8,24,128]{3,2,1,0:T(8,128)S(1)}, f32[8,8,24,128]{3,2,1,0:T(8,128)S(1)}, u32[]{:S(2)}, u32[]{:S(2)}) collective-permute-start(f32[8,8,24,128]{3,2,1,0:T(8,128)S(1)} %convolution_add_fusion.3), channel_id=1, source_target_pairs={{0,1},{1,2},{2,3},{3,4},{4,5},{5,6},{6,7},{7,8},{8,9},{9,10},{10,1... | collective-permute-start | bytes 2359304 | tf_op jit(solution)/shard_map/while/body/eval_jaxpr/ppermute | solution.py:45
  514.9 17.5 %collective-permute-start = (bf16[24,64,128]{2,0,1:T(8,128)(2,1)S(1)}, bf16[24,64,128]{2,0,1:T(8,128)(2,1)S(1)}, u32[]{:S(2)}, u32[]{:S(2)}) collective-permute-start(bf16[24,64,128]{2,0,1:T(8,128)(2,1)S(1)} %copy.136), channel_id=1, source_target_pairs={{0,1},{1,2},{2,3},{3,4},{4,5},{5,6},{6,7},{7,8},{8,9},{9,10},{10,1... | collective-permute-start | bytes 1179656 | tf_op jit(solution)/shard_map/while/body/eval_jaxpr/ppermute | solution.py:45
  551.7 17.6 %collective-permute-start.1 = (f32[8,8,24,128]{3,2,1,0:T(8,128)S(1)}, f32[8,8,24,128]{3,2,1,0:T(8,128)S(1)}, u32[]{:S(2)}, u32[]{:S(2)}) collective-permute-start(f32[8,8,24,128]{3,2,1,0:T(8,128)S(1)} %convolution_add_fusion.3), channel_id=1, source_target_pairs={{0,1},{1,2},{2,3},{3,4},{4,5},{5,6},{6,7},{7,8},{8,9},{9,10},{10,1... | collective-permute-start | bytes 2359304 | tf_op jit(solution)/shard_map/while/body/eval_jaxpr/ppermute | solution.py:45
  551.8 17.5 %collective-permute-start = (bf16[24,64,128]{2,0,1:T(8,128)(2,1)S(1)}, bf16[24,64,128]{2,0,1:T(8,128)(2,1)S(1)}, u32[]{:S(2)}, u32[]{:S(2)}) collective-permute-start(bf16[24,64,128]{2,0,1:T(8,128)(2,1)S(1)} %copy.136), channel_id=1, source_target_pairs={{0,1},{1,2},{2,3},{3,4},{4,5},{5,6},{6,7},{7,8},{8,9},{9,10},{10,1... | collective-permute-start | bytes 1179656 | tf_op jit(solution)/shard_map/while/body/eval_jaxpr/ppermute | solution.py:45
  (50 other events, 574.7 us)
where the time goes:
time: 610 us; the launch traced here: 608 us
  waiting for transfers between devices  274 us (45%)
  matrix products  233 us (38%)
  other arithmetic  59.2 us (10%)
  local copies, waits for them, and re-layouts  31.4 us (5%)
  starting transfers between devices  8.39 us (1%)
    ppermute x60, waiting for transfers between devices, one_step(): return lax.ppermute((q_blk, out_acc, row_max, row_sum), 'cp', send_pairs)  259 us
    dot_general x16, matrix products, absorb(): jnp.einsum('kgts,skd->kgtd', e_cache.astype(jnp.bfloat16), value_cache, p...  116 us
    dot_general x16, matrix products, absorb(): jnp.einsum('tkgd,skd->kgts', q_grouped, key_cache, preferred_element_type...  81.8 us
    reduce_sum x32, other arithmetic, absorb(): row_sum = row_sum * rescale_by + e_cache.sum(axis=-1) + e_fresh.sum(axis=-1)  46.5 us
    dot_general x16, matrix products, absorb(): jnp.einsum('kgts,skd->kgtd', e_fresh.astype(jnp.bfloat16), value_new, pre...  22.3 us
    unnamed x14, local copies, waits for them, and re-layouts  15.7 us
    ppermute x3, waiting for transfers between devices, local_attend(): lax.ppermute((out_acc, row_max, row_sum), 'cp', send_pairs)  14.6 us
    while x45, local copies, waits for them, and re-layouts  14.4 us
  transfers between devices with their start and end apart: 63, of which 32 were waited for; matrix products, arithmetic and copies ran while one was open for 0% of the time, Pallas kernels for 0%

commit v1 on v0

v1 whole, which is shorter than its diff:
```python
import functools

import jax
import jax.numpy as jnp
from jax import lax
from jax.experimental import pallas as pl
from jax.experimental.pallas import tpu as pltpu
from jax.sharding import PartitionSpec as P

NEG = -1e30
LOG2E = 1.4426950408889634
F32 = jnp.float32
BF16 = jnp.bfloat16
TILE = 256
NEW_PAD = 32
SUB = 2048


def _attend(nz, tok, heads, ratio, cache,
            q_hbm, kt_hbm, vt_hbm, kn_hbm, vn_hbm, plen_ref, out_hbm, lse_hbm,
            kbuf, vbuf, knbuf, vnbuf, qbuf, s0, s1, sn0, sn1, bias, qt0, qt1,
            po, plse, rb, rl, outb, lseb,
            kv_loc, kv_send, kv_recv, kn_sem, q_loc, q_send, q_recv,
            ag_send, ag_recv, ro_send, ro_recv, rs_send, rs_recv, out_sem, fin_sem):
    hd = q_hbm.shape[-1]
    scale = hd ** -0.5
    csc = scale * LOG2E
    half = nz // 2
    rows = 2 * tok * ratio
    mine = tok * ratio
    keys = 2 * cache
    per_step = 2 * rows // TILE
    steps = heads * half
    tiles = steps * per_step
    bodies = (tiles + 2) // 2

    rank = lax.axis_index("cp")
    z, c = rank // 2, rank % 2
    partner = 2 * z + (1 - c)
    right = 2 * lax.rem(z + 1, nz) + c
    left = 2 * lax.rem(z + nz - 1, nz) + c
    to = (right, left)

    barrier = pltpu.get_barrier_semaphore()
    for dev in (partner, right, left):
        pl.semaphore_signal(barrier, inc=1, device_id={"cp": dev}, device_id_type=pl.DeviceIdType.MESH)
    pl.semaphore_wait(barrier, 3)

    def remote(src, dst, ss, rs, dev):
        return pltpu.make_async_remote_copy(src_ref=src, dst_ref=dst, send_sem=ss, recv_sem=rs,
                                            device_id={"cp": dev}, device_id_type=pl.DeviceIdType.MESH)

    def q_in(h):
        there = remote(q_hbm.at[heads * (1 - c) + h], qbuf.at[h, 0, pl.ds(c * mine, mine)], q_send.at[h], q_recv.at[h], partner)
        here = pltpu.make_async_copy(q_hbm.at[heads * c + h], qbuf.at[h, 0, pl.ds(c * mine, mine)], q_loc.at[h])
        return there, here

    def kv_in(h):
        out = []
        for n, (src, dst) in enumerate(((kt_hbm, kbuf.at[h, pl.ds(c * cache, cache), :]),
                                        (vt_hbm, vbuf.at[h, :, pl.ds(c * cache, cache)]))):
            out.append((remote(src.at[heads * (1 - c) + h], dst, kv_send.at[n, h], kv_recv.at[n, h], partner),
                        pltpu.make_async_copy(src.at[heads * c + h], dst, kv_loc.at[n, h])))
        return out

    def new_in():
        out = []
        for n, (src, dst) in enumerate(((kn_hbm, knbuf), (vn_hbm, vnbuf))):
            out.append((remote(src.at[pl.ds(heads * (1 - c), heads)], dst.at[c], kn_sem.at[n, 0], kn_sem.at[n, 1], partner),
                        pltpu.make_async_copy(src.at[pl.ds(heads * c, heads)], dst.at[c], kn_sem.at[n, 2])))
        return out

    def q_slot(h, d, k):
        if k == 0:
            return qbuf.at[h, 0, pl.ds(0, rows)]
        if k == half:
            return qbuf.at[h, 0, pl.ds(rows, rows)]
        return qbuf.at[h, k, pl.ds(d * rows, rows)]

    def far_dir(h):
        return h % 2

    def ag(h, d, k):
        return remote(q_slot(h, d, k), q_slot(h, d, k + 1), ag_send.at[d, h, k], ag_recv.at[d, h, k], to[d])

    def ag_start(h, k):
        for d in (0, 1):
            if k + 1 < half or far_dir(h) == d:
                ag(h, d, k).start()

    def ag_wait(h, k):
        for d in (0, 1):
            if k + 1 < half or far_dir(h) == d:
                ag(h, d, k).wait_recv()

    def po_part(h, d, k):
        if k == half:
            sl = pl.ds(rows, rows)
            return po.at[h, 0, :, sl], plse.at[h, 0, :, sl]
        sl = pl.ds((1 - d) * rows, rows)
        return po.at[h, k, :, sl], plse.at[h, k, :, sl]

    def rs(h, d, k):
        o, l = po_part(h, d, k)
        return (remote(o, rb.at[d, h, k - 1], ro_send.at[d, h, k - 1], ro_recv.at[d, h, k - 1], to[d]),
                remote(l, rl.at[d, h, k - 1], rs_send.at[d, h, k - 1], rs_recv.at[d, h, k - 1], to[d]))

    def merge(parts):
        top = functools.reduce(jnp.maximum, [l for _, l in parts])
        ws = [jnp.exp(l - top) for _, l in parts]
        tot = functools.reduce(jnp.add, ws)
        inv = 1.0 / tot
        acc = functools.reduce(jnp.add, [o.astype(F32) * (w * inv) for (o, _), w in zip(parts, ws)])
        return acc, top + jnp.log(tot)

    def rs_stage(h, k):
        for d in (0, 1):
            if k == half and far_dir(h) != d:
                continue
            if k + 1 < half or (k + 1 == half and far_dir(h) == d):
                for cp in rs(h, d, k + 1):
                    cp.wait_recv()
                o, l = po_part(h, d, k)
                acc, lse = merge([(o[...], l[...]), (rb[d, h, k], rl[d, h, k])])
                o[...] = acc.astype(BF16)
                l[...] = lse
            for cp in rs(h, d, k):
                cp.start()

    def out_copies(h):
        there = remote(outb.at[h, pl.ds((1 - c) * mine, mine)], out_hbm.at[heads * c + h], out_sem.at[h, 0], out_sem.at[h, 1], partner)
        here = pltpu.make_async_copy(outb.at[h, pl.ds(c * mine, mine)], out_hbm.at[heads * c + h], out_sem.at[h, 2])
        return there, here

    def final(h):
        for d in (0, 1):
            for cp in rs(h, d, 1):
                cp.wait_recv()
        acc, lse = merge([(po[h, 0, :, 0:rows], plse[h, 0, :, 0:rows])] + [(rb[d, h, 0], rl[d, h, 0]) for d in (0, 1)])
        outb[h] = acc.T.astype(BF16)
        lseb[h:h + 1, :] = lse
        for cp in out_copies(h):
            cp.start()

    def kv_wait(h):
        for there, here in kv_in(h):
            here.wait()
            there.wait_recv()

    for h in range(heads):
        for cp in q_in(h):
            cp.start()
    for there, here in kv_in(0) + new_in():
        there.start()
        here.start()
    for h in range(1, heads):
        for there, here in kv_in(h):
            there.start()
            here.start()

    def q_wait_send(h):
        there, here = q_in(h)
        here.wait()
        there.wait_recv()
        ag_start(h, 0)

    pos = z * keys + lax.broadcasted_iota(jnp.int32, (keys, hd), 0)
    lane = lax.broadcasted_iota(jnp.int32, (keys, hd), 1)
    bias[...] = jnp.where((pos >= plen_ref[0]) & (lane == 0), NEG, 0.0).astype(BF16)
    ones = jnp.where(lax.broadcasted_iota(jnp.int32, (TILE - hd, TILE), 0) == 0, 1.0, 0.0).astype(BF16)
    for r in (qt0, qt1):
        r[hd:TILE, :] = ones
    lseb[...] = jnp.zeros_like(lseb)
    QT, SR, SN = (qt0, qt1), (s0, s1), (sn0, sn1)

    for h in (0, 1):
        q_wait_send(h)

    ev = {i: [] for i in range(bodies + 1)}

    def at(i, f, *a):
        ev[min(i, bodies)].append((f, a))

    def need(s):
        return (3 * s - 1) // 2

    def hop(h, k):
        ag_wait(h, k)
        if k + 1 < half:
            ag_start(h, k + 1)

    for k in range(half):
        at((0, 1, 2, 4)[k], hop, 0, k)
    for k in range(half):
        at((1, 2, 4, 5)[k], hop, 1, k)
    at(3, q_wait_send, 2)
    for k in range(half):
        at((5, 7, 9, 11)[k], hop, 2, k)
    at(9, q_wait_send, 3)
    for k in range(half):
        at((11, 13, 15, 17)[k], hop, 3, k)
    for h in range(1, heads):
        at(6 * h, kv_wait, h)
    for h, when in enumerate(((7, 9, 11, 13, 15), (9, 11, 13, 15, 17), (15, 17, 19, 21, 23), (21, 23, 24, 25, 25))):
        for j, k in enumerate(range(half, 0, -1)):
            at(when[j], rs_stage, h, k)
        at(when[half], final, h)

    def place(t):
        s, n = t // per_step, lax.rem(t, per_step)
        h, r = s // half, lax.rem(s, half)
        pair = jnp.where(h == 0, lax.rem(r + 1, half), lax.rem(half - r, half))
        return h, pair, n

    def make_qt(t, slot):
        h, pair, n = place(jnp.clip(t, 0, tiles - 1))
        q = qbuf[h, pair, pl.ds(pl.multiple_of(n * TILE, TILE), TILE), :]
        QT[slot][0:hd, :] = q.astype(F32).T.astype(BF16)

    def dot(a, b):
        return lax.dot_general(a, b, (((1,), (0,)), ((), ())), preferred_element_type=F32)

    def colmax(x):
        return jnp.max(x.reshape(x.shape[0] // 8, 8, TILE), axis=0)

    def colsum(x):
        return jnp.sum(x.reshape(x.shape[0] // 8, 8, TILE), axis=0)

    def tile(i, mm, par):
        hA, pairA, nA = place(jnp.clip(i + 1, 0, tiles - 1))
        hB, pairB, nB = place(jnp.clip(i, 0, tiles - 1))
        m = jnp.max(mm, axis=0, keepdims=True)
        mc = m * csc
        l = jnp.zeros((8, TILE), F32)
        mm = jnp.full((8, TILE), -jnp.inf, F32)
        acc = None
        for u in range(keys // SUB):
            sl = pl.ds(u * SUB, SUB)
            sv = dot(jnp.concatenate([kbuf[hA, sl, :], bias[sl, :]], axis=1), QT[par][...])
            SR[par][sl, :] = sv
            mm = jnp.maximum(mm, colmax(sv))
            pe = jnp.exp2(SR[1 - par][sl, :] * csc - mc)
            l = l + colsum(pe)
            pv = dot(vbuf[hB, :, sl], pe.astype(BF16))
            acc = pv if acc is None else acc + pv
            if u == 0:
                make_qt(i + 2, 1 - par)
        blk_a = jnp.where(pairA == 0, z, lax.rem(z + nz - pairA, nz))
        blk_b = jnp.where(pairA == 0, lax.rem(z + half, nz), lax.rem(z + pairA, nz))
        tl = (nA * TILE + lax.broadcasted_iota(jnp.int32, (NEW_PAD, TILE), 1)) // ratio
        qtok = jnp.where(tl < 2 * tok, 2 * tok * blk_a + tl, 2 * tok * blk_b + tl - 2 * tok)
        kid = lax.broadcasted_iota(jnp.int32, (NEW_PAD, TILE), 0)
        pn = []
        for q in (0, 1):
            pe = jnp.exp2(SN[1 - par][q] * csc - mc)
            l = l + colsum(pe)
            pn += [pe.astype(BF16), jnp.zeros((128 - NEW_PAD, TILE), BF16)]
            ktok = 2 * tok * z + tok * q + kid
            sv = jnp.where((kid < tok) & (ktok <= qtok), dot(knbuf[q, hA], QT[par][0:hd, :]), NEG)
            SN[par][q] = sv
            mm = jnp.maximum(mm, colmax(sv))
        acc = acc + dot(jnp.concatenate([vnbuf[0, hB], vnbuf[1, hB]], axis=1), jnp.concatenate(pn, axis=0))
        lt = jnp.sum(l, axis=0, keepdims=True)
        sl = pl.ds(pl.multiple_of(nB * TILE, TILE), TILE)
        plse[hB, pairB, :, sl] = m * scale + jnp.log(lt)
        po[hB, pairB, :, sl] = (acc * (1.0 / lt)).astype(BF16)
        return mm

    for f, a in ev[0]:
        f(*a)
    kv_wait(0)
    for there, here in new_in():
        here.wait()
        there.wait_recv()
    make_qt(0, 0)

    def pair_of_tiles(t, mm):
        for i in range(1, bodies):
            if ev[i]:
                @pl.when(t == i)
                def _(i=i):
                    for f, a in ev[i]:
                        f(*a)
        return tile(2 * t, tile(2 * t - 1, mm, 0), 1)

    lax.fori_loop(0, bodies, pair_of_tiles, jnp.zeros((8, TILE), F32))

    for f, a in ev[bodies]:
        f(*a)
    fin = (remote(lseb, lse_hbm.at[c], fin_sem.at[0], fin_sem.at[1], partner),
           pltpu.make_async_copy(lseb, lse_hbm.at[c], fin_sem.at[2]))
    for cp in fin:
        cp.start()

    for h in range(heads):
        q_in(h)[0].wait_send()
        for there, _ in kv_in(h):
            there.wait_send()
        for d in (0, 1):
            for k in range(half):
                if k + 1 < half or far_dir(h) == d:
                    ag(h, d, k).wait_send()
            for k in range(1, half + 1):
                if k < half or far_dir(h) == d:
                    for cp in rs(h, d, k):
                        cp.wait_send()
        there, here = out_copies(h)
        here.wait()
        there.wait()
    for there, _ in new_in():
        there.wait_send()
    fin[1].wait()
    fin[0].wait()


def solution(mesh):
    nz = mesh.shape["cp"] // 2
    tok_spec = P(("dp", "cp"))

    def local(queries, key_new, value_new, key_cache, value_cache, prefix_len):
        tok, nq, hd = queries.shape
        cache, nkv = key_cache.shape[0], key_cache.shape[1]
        ratio = nq // nkv
        heads = nkv // 2
        half = nz // 2
        rank = lax.axis_index("cp")
        c = rank % 2
        ok = (rank * cache + jnp.arange(cache) < prefix_len[0])[:, None, None]
        zero = jnp.zeros((), BF16)
        kt = jnp.where(ok, key_cache, zero).transpose(1, 0, 2)
        vt = jnp.where(ok, value_cache, zero).transpose(1, 2, 0)
        kn = jnp.pad(key_new.transpose(1, 0, 2), ((0, 0), (0, NEW_PAD - tok), (0, 0)))
        vn = jnp.pad(value_new.transpose(1, 2, 0), ((0, 0), (0, 0), (0, 128 - tok)))
        qh = queries.reshape(tok, nkv, ratio, hd).transpose(1, 0, 2, 3).reshape(nkv, tok * ratio, hd)
        rows, mine, keys = 2 * tok * ratio, tok * ratio, 2 * cache
        dma = pltpu.SemaphoreType.DMA
        out, lse = pl.pallas_call(
            functools.partial(_attend, nz, tok, heads, ratio, cache),
            out_shape=(jax.ShapeDtypeStruct((nkv, mine, hd), BF16), jax.ShapeDtypeStruct((2, 8, rows), F32)),
            in_specs=[pl.BlockSpec(memory_space=pl.ANY)] * 5 + [pl.BlockSpec(memory_space=pltpu.SMEM)],
            out_specs=[pl.BlockSpec(memory_space=pl.ANY)] * 2,
            scratch_shapes=[
                pltpu.VMEM((heads, keys, hd), BF16), pltpu.VMEM((heads, hd, keys), BF16),
                pltpu.VMEM((2, heads, NEW_PAD, hd), BF16), pltpu.VMEM((2, heads, hd, 128), BF16),
                pltpu.VMEM((heads, half, 2 * rows, hd), BF16),
                pltpu.VMEM((keys, TILE), F32), pltpu.VMEM((keys, TILE), F32),
                pltpu.VMEM((2, NEW_PAD, TILE), F32), pltpu.VMEM((2, NEW_PAD, TILE), F32),
                pltpu.VMEM((keys, hd), BF16),
                pltpu.VMEM((TILE, TILE), BF16), pltpu.VMEM((TILE, TILE), BF16),
                pltpu.VMEM((heads, half, hd, 2 * rows), BF16), pltpu.VMEM((heads, half, 1, 2 * rows), F32),
                pltpu.VMEM((2, heads, half, hd, rows), BF16), pltpu.VMEM((2, heads, half, 1, rows), F32),
                pltpu.VMEM((heads, rows, hd), BF16), pltpu.VMEM((8, rows), F32),
                dma((2, heads)), dma((2, heads)), dma((2, heads)), dma((2, 3)),
                dma((heads,)), dma((heads,)), dma((heads,)),
                dma((2, heads, half)), dma((2, heads, half)),
                dma((2, heads, half)), dma((2, heads, half)),
                dma((2, heads, half)), dma((2, heads, half)),
                dma((heads, 3)), dma((3,)),
            ],
            compiler_params=pltpu.CompilerParams(collective_id=0, has_side_effects=True, vmem_limit_bytes=60 * 2**20),
            name="ring_attend",
        )(qh, kt, vt, kn, vn, prefix_len)
        attn = out.reshape(nkv, tok, ratio, hd).transpose(1, 0, 2, 3).reshape(tok, nq, hd)
        lse = lse[:, :heads].reshape(nkv, 2, tok, ratio)
        lse = lax.dynamic_index_in_dim(lse, c, axis=1, keepdims=False)
        row_lse = lse.transpose(1, 0, 2).reshape(tok, nq)
        return attn, row_lse

    return jax.shard_map(local, mesh=mesh, in_specs=(tok_spec,) * 5 + (P("dp"),), out_specs=(tok_spec, tok_spec), check_vma=False)
```

time: 610 us -> 148 us (0.24)
  the two profiles are of different devices: /device:TPU:28 before, /device:TPU:21 now
where the time goes in v1:
time: 148 us; the launch traced here: 147 us
  Pallas kernels  113 us (76%)
  local copies, waits for them, and re-layouts  25.8 us (17%)
  other arithmetic  7.29 us (5%)
    pallas_call x1, Pallas kernels, local(): pl.pallas_call(functools.partial(_attend, nz, tok, heads, ratio, cache),...  113 us
    unnamed x11, local copies, waits for them, and re-layouts  14.3 us
    transpose x1, other arithmetic, local(): vt = jnp.where(ok, value_cache, zero).transpose(1, 2, 0)  7.29 us
    transpose x1, local copies, waits for them, and re-layouts, local(): kt = jnp.where(ok, key_cache, zero).transpose(1, 0, 2)  6.48 us

profile of v1, /device:TPU:21, one launch (start us, length us, event | category | flops | bytes accessed | tf_op | source)
XLA Modules:
  0.0 147.5 jit_solution(8503235335093004743)
XLA Ops:
  0.6 0.0 copy-start
  1.4 6.7 %copy.16 = bf16[2048,8,128]{0,2,1:T(8,128)(2,1)} copy(bf16[2048,8,128]{2,1,0:T(8,128)(2,1)} %param.9) | data formatting | bytes 8388608 | tf_op args[3]
  8.1 6.7 %copy.17 = bf16[2048,8,128]{0,2,1:T(8,128)(2,1)} copy(bf16[2048,8,128]{2,1,0:T(8,128)(2,1)} %param.10) | data formatting | bytes 8388608 | tf_op args[4]
  14.7 7.3 %select_bitcast_fusion = (bf16[8,128,2048]{2,1,0:T(8,128)(2,1)}, bf16[8,2048,128]{1,2,0:T(8,128)(2,1)}) fusion(bf16[2048,8,128]{0,2,1:T(8,128)(2,1)} %copy.17, pred[2048]{0:T(1024)(128)(4,1)S(1)} %add_compare_fusion, bf16[2048,8,128]{0,2,1:T(8,128)(2,1)} %copy.16), kind=kLoop, calls=%fused_computation | loop fusion | flops 4194304 | bytes 16779264 | tf_op jit(solution)/shard_map/transpose | solution.py:331
  22.0 0.0 copy-start.1
  22.0 0.0 copy-start.2
  22.0 6.5 %copy.20.kt_hbm = bf16[8,2048,128]{2,1,0:T(8,128)(2,1)} copy(bf16[8,2048,128]{1,2,0:T(8,128)(2,1)} %get-tuple-element.9) | data formatting | bytes 8388608 | tf_op jit(solution)/shard_map/transpose | solution.py:330
  28.5 0.0 copy-done.1
  28.5 0.2 copy.19
  28.7 0.8 pad.9.vn_hbm
  29.5 0.0 copy-done
  29.5 0.8 copy_bitcast_fusion.1.q_hbm
  30.3 0.0 copy-done.2
  30.3 0.6 pad.8.kn_hbm
  31.0 113.0 %ring_attend.1 = (bf16[8,192,128]{2,1,0:T(8,128)(2,1)}, f32[2,8,384]{2,1,0:T(8,128)}) custom-call(bf16[8,192,128]{2,1,0:T(8,128)(2,1)} %copy_bitcast_fusion.1.q_hbm, bf16[8,2048,128]{2,1,0:T(8,128)(2,1)} %copy.20.kt_hbm, bf16[8,128,2048]{2,1,0:T(8,128)(2,1)} %get-tuple-element.8.vt_hbm, bf16[8,32,128]{2,1,0:T(8,128)(2,1)} %pad.8.kn_hbm, ...), custom_call_target="tpu_custom_call" | custom-call | tf_op jit(solution)/shard_map/ring_attend/pallas_call | solution.py:337
  143.9 0.7 slice.3
  144.7 0.1 reshape.31
  144.8 0.1 copy.22
  144.9 0.7 copy.23
  145.6 1.8 %copy_bitcast_fusion = bf16[24,64,128]{2,1,0:T(8,128)(2,1)} fusion(bf16[8,192,128]{2,1,0:T(8,128)(2,1)} %get-tuple-element.4), kind=kLoop, calls=%fused_computation.2 | loop fusion | bytes 786432 | tf_op jit(solution)/shard_map/reshape | solution.py:363
  (3 shorter events, 0.0 us)
Async XLA Ops:
  0.6 28.9 %copy-start = (bf16[24,64,128]{2,1,0:T(8,128)(2,1)S(1)}, bf16[24,64,128]{2,1,0:T(8,128)(2,1)}, u32[]{:S(2)}) copy-start(bf16[24,64,128]{2,1,0:T(8,128)(2,1)} %param.6) | copy-start | bytes 1179652
  22.0 6.5 %copy-start.1 = (bf16[24,8,128]{2,1,0:T(8,128)(2,1)S(1)}, bf16[24,8,128]{2,1,0:T(8,128)(2,1)}, u32[]{:S(2)}) copy-start(bf16[24,8,128]{2,1,0:T(8,128)(2,1)} %param.8) | copy-start | bytes 147460
  22.0 8.3 %copy-start.2 = (bf16[24,8,128]{2,1,0:T(8,128)(2,1)S(1)}, bf16[24,8,128]{2,1,0:T(8,128)(2,1)}, u32[]{:S(2)}) copy-start(bf16[24,8,128]{2,1,0:T(8,128)(2,1)} %param.7) | copy-start | bytes 147460

commit v2 on v1

--- a/solution.py
+++ b/solution.py
@@ -14,13 +14,14 @@
 TILE = 256
 NEW_PAD = 32
 SUB = 2048
+CHUNK = 256
 
 
 def _attend(nz, tok, heads, ratio, cache,
-            q_hbm, kt_hbm, vt_hbm, kn_hbm, vn_hbm, plen_ref, out_hbm, lse_hbm,
+            q_hbm, k_hbm, v_hbm, kn_hbm, vn_hbm, plen_ref, out_hbm, lse_hbm,
             kbuf, vbuf, knbuf, vnbuf, qbuf, s0, s1, sn0, sn1, bias, qt0, qt1,
-            po, plse, rb, rl, outb, lseb,
-            kv_loc, kv_send, kv_recv, kn_sem, q_loc, q_send, q_recv,
+            po, plse, rb, rl, outb, lseb, rawk, rawv, st, ksend, vsend,
+            raw_sem, kv_send, kv_recv, kn_sem, q_loc, q_send, q_recv,
             ag_send, ag_recv, ro_send, ro_recv, rs_send, rs_recv, out_sem, fin_sem):
     hd = q_hbm.shape[-1]
     scale = hd ** -0.5
@@ -50,18 +51,44 @@
         return pltpu.make_async_remote_copy(src_ref=src, dst_ref=dst, send_sem=ss, recv_sem=rs,
                                             device_id={"cp": dev}, device_id_type=pl.DeviceIdType.MESH)
 
+    def head_rows(ref, n):
+        return ref.at[:, pl.ds(pl.multiple_of(n * ratio, ratio), ratio), :]
+
     def q_in(h):
-        there = remote(q_hbm.at[heads * (1 - c) + h], qbuf.at[h, 0, pl.ds(c * mine, mine)], q_send.at[h], q_recv.at[h], partner)
-        here = pltpu.make_async_copy(q_hbm.at[heads * c + h], qbuf.at[h, 0, pl.ds(c * mine, mine)], q_loc.at[h])
+        dst = qbuf.at[h, 0, pl.ds(c * tok, tok)]
+        there = remote(head_rows(q_hbm, heads * (1 - c) + h), dst, q_send.at[h], q_recv.at[h], partner)
+        here = pltpu.make_async_copy(head_rows(q_hbm, heads * c + h), dst, q_loc.at[h])
         return there, here
 
+    def raw_in():
+        return [pltpu.make_async_copy(src, dst, raw_sem.at[n]) for n, (src, dst) in enumerate(((k_hbm, rawk), (v_hbm, rawv)))]
+
     def kv_in(h):
-        out = []
-        for n, (src, dst) in enumerate(((kt_hbm, kbuf.at[h, pl.ds(c * cache, cache), :]),
-                                        (vt_hbm, vbuf.at[h, :, pl.ds(c * cache, cache)]))):
-            out.append((remote(src.at[heads * (1 - c) + h], dst, kv_send.at[n, h], kv_recv.at[n, h], partner),
-                        pltpu.make_async_copy(src.at[heads * c + h], dst, kv_loc.at[n, h])))
-        return out
+        return [remote(ksend.at[h], kbuf.at[h, pl.ds(c * cache, cache), :], kv_send.at[0, h], kv_recv.at[0, h], partner),
+                remote(vsend.at[h], vbuf.at[h, :, pl.ds(c * cache, cache)], kv_send.at[1, h], kv_recv.at[1, h], partner)]
+
+    def relayout(raw, put):
+        def chunk(i, _):
+            st[...] = raw[pl.ds(pl.multiple_of(i * CHUNK * 2 * heads, CHUNK * 2 * heads), CHUNK * 2 * heads), :].astype(F32)
+            ok = rank * cache + i * CHUNK + lax.broadcasted_iota(jnp.int32, (CHUNK, hd), 0) < plen_ref[0]
+            at0 = pl.multiple_of(i * CHUNK, CHUNK)
+            for h in range(heads):
+                for own, n in ((True, heads * c + h), (False, heads * (1 - c) + h)):
+                    put(own, h, at0, jnp.where(ok, st[pl.ds(n, CHUNK, stride=2 * heads), :], 0.0))
+            return 0
+        lax.fori_loop(0, cache // CHUNK, chunk, 0)
+
+    def put_k(own, h, at0, x):
+        if own:
+            kbuf[h, pl.ds(pl.multiple_of(c * cache + at0, CHUNK), CHUNK), :] = x.astype(BF16)
+        else:
+            ksend[h, pl.ds(at0, CHUNK), :] = x.astype(BF16)
+
+    def put_v(own, h, at0, x):
+        if own:
+            vbuf[h, :, pl.ds(pl.multiple_of(c * cache + at0, CHUNK), CHUNK)] = x.T.astype(BF16)
+        else:
+            vsend[h, :, pl.ds(at0, CHUNK)] = x.T.astype(BF16)
 
     def new_in():
         out = []
@@ -72,10 +99,10 @@
 
     def q_slot(h, d, k):
         if k == 0:
-            return qbuf.at[h, 0, pl.ds(0, rows)]
+            return qbuf.at[h, 0, pl.ds(0, 2 * tok)]
         if k == half:
-            return qbuf.at[h, 0, pl.ds(rows, rows)]
-        return qbuf.at[h, k, pl.ds(d * rows, rows)]
+            return qbuf.at[h, 0, pl.ds(2 * tok, 2 * tok)]
+        return qbuf.at[h, k, pl.ds(d * 2 * tok, 2 * tok)]
 
     def far_dir(h):
         return h % 2
@@ -92,6 +119,11 @@
         for d in (0, 1):
             if k + 1 < half or far_dir(h) == d:
                 ag(h, d, k).wait_recv()
+
+    def hop(h, k):
+        ag_wait(h, k)
+        if k + 1 < half:
+            ag_start(h, k + 1)
 
     def po_part(h, d, k):
         if k == half:
@@ -128,8 +160,9 @@
                 cp.start()
 
     def out_copies(h):
-        there = remote(outb.at[h, pl.ds((1 - c) * mine, mine)], out_hbm.at[heads * c + h], out_sem.at[h, 0], out_sem.at[h, 1], partner)
-        here = pltpu.make_async_copy(outb.at[h, pl.ds(c * mine, mine)], out_hbm.at[heads * c + h], out_sem.at[h, 2])
+        dst = head_rows(out_hbm, heads * c + h)
+        there = remote(outb.at[h, pl.ds((1 - c) * tok, tok)], dst, out_sem.at[h, 0], out_sem.at[h, 1], partner)
+        here = pltpu.make_async_copy(outb.at[h, pl.ds(c * tok, tok)], dst, out_sem.at[h, 2])
         return there, here
 
     def final(h):
@@ -137,26 +170,23 @@
             for cp in rs(h, d, 1):
                 cp.wait_recv()
         acc, lse = merge([(po[h, 0, :, 0:rows], plse[h, 0, :, 0:rows])] + [(rb[d, h, 0], rl[d, h, 0]) for d in (0, 1)])
-        outb[h] = acc.T.astype(BF16)
+        outb[h] = acc.T.reshape(2 * tok, ratio, hd).astype(BF16)
         lseb[h:h + 1, :] = lse
         for cp in out_copies(h):
             cp.start()
 
     def kv_wait(h):
-        for there, here in kv_in(h):
-            here.wait()
+        for there in kv_in(h):
             there.wait_recv()
 
     for h in range(heads):
         for cp in q_in(h):
             cp.start()
-    for there, here in kv_in(0) + new_in():
+    for cp in raw_in():
+        cp.start()
+    for there, here in new_in():
         there.start()
         here.start()
-    for h in range(1, heads):
-        for there, here in kv_in(h):
-            there.start()
-            here.start()
 
     def q_wait_send(h):
         there, here = q_in(h)
@@ -175,6 +205,15 @@
 
     for h in (0, 1):
         q_wait_send(h)
+    raw_in()[0].wait()
+    relayout(rawk, put_k)
+    for h in range(heads):
+        kv_in(h)[0].start()
+    hop(0, 0)
+    raw_in()[1].wait()
+    relayout(rawv, put_v)
+    for h in range(heads):
+        kv_in(h)[1].start()
 
     ev = {i: [] for i in range(bodies + 1)}
 
@@ -184,12 +223,7 @@
     def need(s):
         return (3 * s - 1) // 2
 
-    def hop(h, k):
-        ag_wait(h, k)
-        if k + 1 < half:
-            ag_start(h, k + 1)
-
-    for k in range(half):
+    for k in range(1, half):
         at((0, 1, 2, 4)[k], hop, 0, k)
     for k in range(half):
         at((1, 2, 4, 5)[k], hop, 1, k)
@@ -214,8 +248,8 @@
 
     def make_qt(t, slot):
         h, pair, n = place(jnp.clip(t, 0, tiles - 1))
-        q = qbuf[h, pair, pl.ds(pl.multiple_of(n * TILE, TILE), TILE), :]
-        QT[slot][0:hd, :] = q.astype(F32).T.astype(BF16)
+        q = qbuf[h, pair, pl.ds(n * (TILE // ratio), TILE // ratio)].astype(F32).reshape(TILE, hd)
+        QT[slot][0:hd, :] = q.T.astype(BF16)
 
     def dot(a, b):
         return lax.dot_general(a, b, (((1,), (0,)), ((), ())), preferred_element_type=F32)
@@ -294,7 +328,7 @@
 
     for h in range(heads):
         q_in(h)[0].wait_send()
-        for there, _ in kv_in(h):
+        for there in kv_in(h):
             there.wait_send()
         for d in (0, 1):
             for k in range(half):
@@ -325,32 +359,29 @@
         half = nz // 2
         rank = lax.axis_index("cp")
         c = rank % 2
-        ok = (rank * cache + jnp.arange(cache) < prefix_len[0])[:, None, None]
-        zero = jnp.zeros((), BF16)
-        kt = jnp.where(ok, key_cache, zero).transpose(1, 0, 2)
-        vt = jnp.where(ok, value_cache, zero).transpose(1, 2, 0)
         kn = jnp.pad(key_new.transpose(1, 0, 2), ((0, 0), (0, NEW_PAD - tok), (0, 0)))
         vn = jnp.pad(value_new.transpose(1, 2, 0), ((0, 0), (0, 0), (0, 128 - tok)))
-        qh = queries.reshape(tok, nkv, ratio, hd).transpose(1, 0, 2, 3).reshape(nkv, tok * ratio, hd)
-        rows, mine, keys = 2 * tok * ratio, tok * ratio, 2 * cache
+        rows, keys = 2 * tok * ratio, 2 * cache
         dma = pltpu.SemaphoreType.DMA
         out, lse = pl.pallas_call(
             functools.partial(_attend, nz, tok, heads, ratio, cache),
-            out_shape=(jax.ShapeDtypeStruct((nkv, mine, hd), BF16), jax.ShapeDtypeStruct((2, 8, rows), F32)),
+            out_shape=(jax.ShapeDtypeStruct((tok, nq, hd), BF16), jax.ShapeDtypeStruct((2, 8, rows), F32)),
             in_specs=[pl.BlockSpec(memory_space=pl.ANY)] * 5 + [pl.BlockSpec(memory_space=pltpu.SMEM)],
             out_specs=[pl.BlockSpec(memory_space=pl.ANY)] * 2,
             scratch_shapes=[
                 pltpu.VMEM((heads, keys, hd), BF16), pltpu.VMEM((heads, hd, keys), BF16),
                 pltpu.VMEM((2, heads, NEW_PAD, hd), BF16), pltpu.VMEM((2, heads, hd, 128), BF16),
-                pltpu.VMEM((heads, half, 2 * rows, hd), BF16),
+                pltpu.VMEM((heads, half, 4 * tok, ratio, hd), BF16),
                 pltpu.VMEM((keys, TILE), F32), pltpu.VMEM((keys, TILE), F32),
                 pltpu.VMEM((2, NEW_PAD, TILE), F32), pltpu.VMEM((2, NEW_PAD, TILE), F32),
                 pltpu.VMEM((keys, hd), BF16),
                 pltpu.VMEM((TILE, TILE), BF16), pltpu.VMEM((TILE, TILE), BF16),
                 pltpu.VMEM((heads, half, hd, 2 * rows), BF16), pltpu.VMEM((heads, half, 1, 2 * rows), F32),
                 pltpu.VMEM((2, heads, half, hd, rows), BF16), pltpu.VMEM((2, heads, half, 1, rows), F32),
-                pltpu.VMEM((heads, rows, hd), BF16), pltpu.VMEM((8, rows), F32),
-                dma((2, heads)), dma((2, heads)), dma((2, heads)), dma((2, 3)),
+                pltpu.VMEM((heads, 2 * tok, ratio, hd), BF16), pltpu.VMEM((8, rows), F32),
+                pltpu.VMEM((cache * nkv, hd), BF16), pltpu.VMEM((cache * nkv, hd), BF16), pltpu.VMEM((CHUNK * nkv, hd), F32),
+                pltpu.VMEM((heads, cache, hd), BF16), pltpu.VMEM((heads, hd, cache), BF16),
+                dma((2,)), dma((2, heads)), dma((2, heads)), dma((2, 3)),
                 dma((heads,)), dma((heads,)), dma((heads,)),
                 dma((2, heads, half)), dma((2, heads, half)),
                 dma((2, heads, half)), dma((2, heads, half)),
@@ -359,11 +390,10 @@
             ],
             compiler_params=pltpu.CompilerParams(collective_id=0, has_side_effects=True, vmem_limit_bytes=60 * 2**20),
             name="ring_attend",
-        )(qh, kt, vt, kn, vn, prefix_len)
-        attn = out.reshape(nkv, tok, ratio, hd).transpose(1, 0, 2, 3).reshape(tok, nq, hd)
+        )(queries, key_cache.reshape(cache * nkv, hd), value_cache.reshape(cache * nkv, hd), kn, vn, prefix_len)
         lse = lse[:, :heads].reshape(nkv, 2, tok, ratio)
         lse = lax.dynamic_index_in_dim(lse, c, axis=1, keepdims=False)
         row_lse = lse.transpose(1, 0, 2).reshape(tok, nq)
-        return attn, row_lse
+        return out, row_lse
 
     return jax.shard_map(local, mesh=mesh, in_specs=(tok_spec,) * 5 + (P("dp"),), out_specs=(tok_spec, tok_spec), check_vma=False)

time: 148 us -> 127 us (0.86)
  local copies, waits for them, and re-layouts: 25.8 us -> 6.59 us
  other arithmetic: 7.29 us -> 0 us
  Pallas kernels: 113 us -> 119 us
    unnamed x11 -> x4, local copies, waits for them, and re-layouts: 14.3 us -> 4.24 us
    transpose x1 -> x0, other arithmetic: 7.29 us -> none  [local(): vt = jnp.where(ok, value_cache, zero).transpose(1, 2, 0)]
    transpose x1 -> x0, local copies, waits for them, and re-layouts: 6.48 us -> none  [local(): kt = jnp.where(ok, key_cache, zero).transpose(1, 0, 2)]
    pallas_call x1, Pallas kernels: 113 us -> 119 us  [local(): pl.pallas_call(functools.partial(_attend, nz, tok, heads, ratio, cache),...]
    reshape x2 -> x0, local copies, waits for them, and re-layouts: 2.67 us -> none  [the longest x1 1.85 us: local(): out.reshape(nkv, tok, ratio, hd).transpose(1, 0, 2, 3).reshape(tok, nq, hd)]
where the time goes in v2:
time: 127 us
  Pallas kernels  119 us (94%)
  local copies, waits for them, and re-layouts  6.59 us (5%)
  between operations  1.33 us (1%)
    pallas_call x1, Pallas kernels, local(): pl.pallas_call(functools.partial(_attend, nz, tok, heads, ratio, cache),...  119 us
    unnamed x4, local copies, waits for them, and re-layouts  4.24 us

profile of v2, /device:TPU:21, one launch (start us, length us, event | category | flops | bytes accessed | tf_op | source)
XLA Modules:
  0.0 127.0 jit_solution(7141490202894017908)
XLA Ops:
  0.6 1.0 copy.11
  1.6 0.8 pad.9.vn_hbm
  2.4 0.8 copy.15
  3.2 0.6 pad.8.kn_hbm
  4.5 119.1 %ring_attend.1 = (bf16[24,64,128]{2,1,0:T(8,128)(2,1)}, f32[2,8,384]{2,1,0:T(8,128)}) custom-call(bf16[24,64,128]{2,1,0:T(8,128)(2,1)} %q_hbm.1, bf16[16384,128]{1,0:T(8,128)(2,1)} %bitcast.11, bf16[16384,128]{1,0:T(8,128)(2,1)} %bitcast.12, bf16[8,32,128]{2,1,0:T(8,128)(2,1)} %pad.8.kn_hbm, bf16[8,128,128]{2,1,0:T(8,128)(2,1)} %pad.9.vn_hbm, ...), custom_call_target="tpu_custom_call" | custom-call | tf_op jit(solution)/shard_map/ring_attend/pallas_call | solution.py:366
  123.6 0.7 slice.3
  124.3 0.1 reshape.18
  124.5 0.1 copy.12
  124.6 0.7 copy.13
  125.3 1.8 %copy.18 = bf16[24,64,128]{2,1,0:T(8,128)(2,1)} copy(bf16[24,64,128]{2,1,0:T(8,128)(2,1)} %get-tuple-element.10) | data formatting | bytes 786432
  (1 shorter events, 0.0 us)

commit v3 on v2

--- a/solution.py
+++ b/solution.py
@@ -20,7 +20,7 @@
 def _attend(nz, tok, heads, ratio, cache,
             q_hbm, k_hbm, v_hbm, kn_hbm, vn_hbm, plen_ref, out_hbm, lse_hbm,
             kbuf, vbuf, knbuf, vnbuf, qbuf, s0, s1, sn0, sn1, bias, qt0, qt1,
-            po, plse, rb, rl, outb, lseb, rawk, rawv, st, ksend, vsend,
+            po, plse, rb, rl, outb, lseb, rawk, rawv, st, ksend, vsend, rawn, knsend, vnsend,
             raw_sem, kv_send, kv_recv, kn_sem, q_loc, q_send, q_recv,
             ag_send, ag_recv, ro_send, ro_recv, rs_send, rs_recv, out_sem, fin_sem):
     hd = q_hbm.shape[-1]
@@ -33,7 +33,7 @@
     per_step = 2 * rows // TILE
     steps = heads * half
     tiles = steps * per_step
-    bodies = (tiles + 2) // 2
+    bodies = tiles // 2
 
     rank = lax.axis_index("cp")
     z, c = rank // 2, rank % 2
@@ -90,12 +90,25 @@
         else:
             vsend[h, :, pl.ds(at0, CHUNK)] = x.T.astype(BF16)
 
+    def new_raw():
+        return [pltpu.make_async_copy(src, rawn.at[n], kn_sem.at[n, 2]) for n, src in enumerate((kn_hbm, vn_hbm))]
+
     def new_in():
-        out = []
-        for n, (src, dst) in enumerate(((kn_hbm, knbuf), (vn_hbm, vnbuf))):
-            out.append((remote(src.at[pl.ds(heads * (1 - c), heads)], dst.at[c], kn_sem.at[n, 0], kn_sem.at[n, 1], partner),
-                        pltpu.make_async_copy(src.at[pl.ds(heads * c, heads)], dst.at[c], kn_sem.at[n, 2])))
-        return out
+        return [remote(src, dst.at[c], kn_sem.at[n, 0], kn_sem.at[n, 1], partner)
+                for n, (src, dst) in enumerate(((knsend, knbuf), (vnsend, vnbuf)))]
+
+    def relayout_new():
+        for n, (pad, mine, theirs) in enumerate(((NEW_PAD, knbuf, knsend), (hd, vnbuf, vnsend))):
+            st[0:tok * 2 * heads, :] = rawn[n].astype(F32)
+            for h in range(heads):
+                for own, src in ((True, heads * c + h), (False, heads * (1 - c) + h)):
+                    x = st[pl.ds(src, tok, stride=2 * heads), :]
+                    x = jnp.concatenate([x, jnp.zeros((pad - tok, hd), F32)], axis=0)
+                    x = (x if n == 0 else x.T).astype(BF16)
+                    if own:
+                        mine[c, h] = x
+                    else:
+                        theirs[h] = x
 
     def q_slot(h, d, k):
         if k == 0:
@@ -184,9 +197,8 @@
             cp.start()
     for cp in raw_in():
         cp.start()
-    for there, here in new_in():
-        there.start()
-        here.start()
+    for cp in new_raw():
+        cp.start()
 
     def q_wait_send(h):
         there, here = q_in(h)
@@ -205,6 +217,11 @@
 
     for h in (0, 1):
         q_wait_send(h)
+    for cp in new_raw():
+        cp.wait()
+    relayout_new()
+    for cp in new_in():
+        cp.start()
     raw_in()[0].wait()
     relayout(rawk, put_k)
     for h in range(heads):
@@ -220,30 +237,27 @@
     def at(i, f, *a):
         ev[min(i, bodies)].append((f, a))
 
-    def need(s):
-        return (3 * s - 1) // 2
-
-    for k in range(1, half):
-        at((0, 1, 2, 4)[k], hop, 0, k)
-    for k in range(half):
-        at((1, 2, 4, 5)[k], hop, 1, k)
-    at(3, q_wait_send, 2)
-    for k in range(half):
-        at((5, 7, 9, 11)[k], hop, 2, k)
-    at(9, q_wait_send, 3)
-    for k in range(half):
-        at((11, 13, 15, 17)[k], hop, 3, k)
-    for h in range(1, heads):
-        at(6 * h, kv_wait, h)
-    for h, when in enumerate(((7, 9, 11, 13, 15), (9, 11, 13, 15, 17), (15, 17, 19, 21, 23), (21, 23, 24, 25, 25))):
-        for j, k in enumerate(range(half, 0, -1)):
-            at(when[j], rs_stage, h, k)
-        at(when[half], final, h)
+    table = {
+        0: [(q_wait_send, 3), (hop, 1, 0)], 1: [(q_wait_send, 2)], 2: [(hop, 0, 1)], 3: [(hop, 1, 1)],
+        4: [(hop, 0, 2), (hop, 2, 0), (hop, 3, 0)], 6: [(hop, 0, 3), (hop, 1, 2)], 7: [(hop, 2, 1)], 8: [(hop, 3, 1)],
+        9: [(hop, 1, 3), (hop, 2, 2)], 11: [(rs_stage, 0, 4), (hop, 2, 3)], 12: [(hop, 3, 2), (rs_stage, 1, 4)],
+        14: [(rs_stage, 2, 4), (rs_stage, 0, 3)], 15: [(rs_stage, 1, 3)], 16: [(rs_stage, 2, 3), (hop, 3, 3)],
+        18: [(rs_stage, 0, 2)], 19: [(rs_stage, 2, 2)], 20: [(rs_stage, 3, 4), (rs_stage, 1, 2)],
+        21: [(rs_stage, 2, 1), (rs_stage, 3, 3)], 22: [(rs_stage, 0, 1)], 23: [(rs_stage, 3, 2), (rs_stage, 1, 1), (final, 2)],
+        24: [(rs_stage, 3, 1), (final, 0), (final, 1), (final, 3)],
+    }
+    for i, fs in table.items():
+        for f, *a in fs:
+            at(i, f, *a)
+    at(0, kv_wait, 1)
+    at(11, kv_wait, 2)
+    at(17, kv_wait, 3)
 
     def place(t):
         s, n = t // per_step, lax.rem(t, per_step)
-        h, r = s // half, lax.rem(s, half)
-        pair = jnp.where(h == 0, lax.rem(r + 1, half), lax.rem(half - r, half))
+        early = s < 2 * half
+        h = jnp.where(early, lax.rem(s, 2), s // half)
+        pair = jnp.where(early, lax.rem(s // 2 + 1, half), lax.rem(2 * half - lax.rem(s, half), half))
         return h, pair, n
 
     def make_qt(t, slot):
@@ -260,53 +274,64 @@
     def colsum(x):
         return jnp.sum(x.reshape(x.shape[0] // 8, 8, TILE), axis=0)
 
+    def scores(t, par, mm, u):
+        h, pair, n = place(jnp.clip(t, 0, tiles - 1))
+        sl = pl.ds(u * SUB, SUB)
+        lhs = jnp.concatenate([kbuf[h, sl, :], bias[sl, :]], axis=1)
+        if u == 0:
+            kn = jnp.concatenate([knbuf[0, h], knbuf[1, h]], axis=0)
+            lhs = jnp.concatenate([lhs, jnp.concatenate([kn, jnp.zeros((2 * NEW_PAD, TILE - hd), BF16)], axis=1)], axis=0)
+        sv = dot(lhs, QT[par][...])
+        if u == 0:
+            blk_a = jnp.where(pair == 0, z, lax.rem(z + nz - pair, nz))
+            blk_b = jnp.where(pair == 0, lax.rem(z + half, nz), lax.rem(z + pair, nz))
+            tl = lax.shift_right_logical(n * TILE + lax.broadcasted_iota(jnp.int32, (NEW_PAD, TILE), 1), ratio.bit_length() - 1)
+            last = jnp.where(tl < 2 * tok, 2 * tok * (blk_a - z) + tl, 2 * tok * (blk_b - z - 1) + tl)
+            kid = lax.broadcasted_iota(jnp.int32, (NEW_PAD, TILE), 0)
+            for q in (0, 1):
+                x = jnp.where((kid < tok) & (kid + tok * q <= last), sv[SUB + q * NEW_PAD:SUB + (q + 1) * NEW_PAD], NEG)
+                SN[par][q] = x
+                mm = jnp.maximum(mm, colmax(x))
+            sv = sv[:SUB]
+        SR[par][sl, :] = sv
+        return jnp.maximum(mm, colmax(sv))
+
     def tile(i, mm, par):
-        hA, pairA, nA = place(jnp.clip(i + 1, 0, tiles - 1))
-        hB, pairB, nB = place(jnp.clip(i, 0, tiles - 1))
+        h, pair, n = place(i)
         m = jnp.max(mm, axis=0, keepdims=True)
         mc = m * csc
+        mm = jnp.full((8, TILE), -jnp.inf, F32)
         l = jnp.zeros((8, TILE), F32)
-        mm = jnp.full((8, TILE), -jnp.inf, F32)
-        acc = None
-        for u in range(keys // SUB):
-            sl = pl.ds(u * SUB, SUB)
-            sv = dot(jnp.concatenate([kbuf[hA, sl, :], bias[sl, :]], axis=1), QT[par][...])
-            SR[par][sl, :] = sv
-            mm = jnp.maximum(mm, colmax(sv))
-            pe = jnp.exp2(SR[1 - par][sl, :] * csc - mc)
-            l = l + colsum(pe)
-            pv = dot(vbuf[hB, :, sl], pe.astype(BF16))
-            acc = pv if acc is None else acc + pv
-            if u == 0:
-                make_qt(i + 2, 1 - par)
-        blk_a = jnp.where(pairA == 0, z, lax.rem(z + nz - pairA, nz))
-        blk_b = jnp.where(pairA == 0, lax.rem(z + half, nz), lax.rem(z + pairA, nz))
-        tl = (nA * TILE + lax.broadcasted_iota(jnp.int32, (NEW_PAD, TILE), 1)) // ratio
-        qtok = jnp.where(tl < 2 * tok, 2 * tok * blk_a + tl, 2 * tok * blk_b + tl - 2 * tok)
-        kid = lax.broadcasted_iota(jnp.int32, (NEW_PAD, TILE), 0)
         pn = []
         for q in (0, 1):
             pe = jnp.exp2(SN[1 - par][q] * csc - mc)
             l = l + colsum(pe)
             pn += [pe.astype(BF16), jnp.zeros((128 - NEW_PAD, TILE), BF16)]
-            ktok = 2 * tok * z + tok * q + kid
-            sv = jnp.where((kid < tok) & (ktok <= qtok), dot(knbuf[q, hA], QT[par][0:hd, :]), NEG)
-            SN[par][q] = sv
-            mm = jnp.maximum(mm, colmax(sv))
-        acc = acc + dot(jnp.concatenate([vnbuf[0, hB], vnbuf[1, hB]], axis=1), jnp.concatenate(pn, axis=0))
+        acc = dot(jnp.concatenate([vnbuf[0, h], vnbuf[1, h]], axis=1), jnp.concatenate(pn, axis=0))
+        for u in range(keys // SUB):
+            sl = pl.ds(u * SUB, SUB)
+            mm = scores(i + 1, par, mm, u)
+            if u == 0:
+                make_qt(i + 2, 1 - par)
+            pe = jnp.exp2(SR[1 - par][sl, :] * csc - mc)
+            l = l + colsum(pe)
+            acc = acc + dot(vbuf[h, :, sl], pe.astype(BF16))
         lt = jnp.sum(l, axis=0, keepdims=True)
-        sl = pl.ds(pl.multiple_of(nB * TILE, TILE), TILE)
-        plse[hB, pairB, :, sl] = m * scale + jnp.log(lt)
-        po[hB, pairB, :, sl] = (acc * (1.0 / lt)).astype(BF16)
+        sl = pl.ds(pl.multiple_of(n * TILE, TILE), TILE)
+        plse[h, pair, :, sl] = m * scale + jnp.log(lt)
+        po[h, pair, :, sl] = (acc * (1.0 / lt)).astype(BF16)
         return mm
 
+    kv_wait(0)
+    for cp in new_in():
+        cp.wait_recv()
+    make_qt(0, 0)
+    first = jnp.full((8, TILE), -jnp.inf, F32)
+    for u in range(keys // SUB):
+        first = scores(0, 0, first, u)
+    make_qt(1, 1)
     for f, a in ev[0]:
         f(*a)
-    kv_wait(0)
-    for there, here in new_in():
-        here.wait()
-        there.wait_recv()
-    make_qt(0, 0)
 
     def pair_of_tiles(t, mm):
         for i in range(1, bodies):
@@ -315,9 +340,9 @@
                 def _(i=i):
                     for f, a in ev[i]:
                         f(*a)
-        return tile(2 * t, tile(2 * t - 1, mm, 0), 1)
-
-    lax.fori_loop(0, bodies, pair_of_tiles, jnp.zeros((8, TILE), F32))
+        return tile(2 * t + 1, tile(2 * t, mm, 1), 0)
+
+    lax.fori_loop(0, bodies, pair_of_tiles, first)
 
     for f, a in ev[bodies]:
         f(*a)
@@ -341,8 +366,8 @@
         there, here = out_copies(h)
         here.wait()
         there.wait()
-    for there, _ in new_in():
-        there.wait_send()
+    for cp in new_in():
+        cp.wait_send()
     fin[1].wait()
     fin[0].wait()
 
@@ -359,8 +384,6 @@
         half = nz // 2
         rank = lax.axis_index("cp")
         c = rank % 2
-        kn = jnp.pad(key_new.transpose(1, 0, 2), ((0, 0), (0, NEW_PAD - tok), (0, 0)))
-        vn = jnp.pad(value_new.transpose(1, 2, 0), ((0, 0), (0, 0), (0, 128 - tok)))
         rows, keys = 2 * tok * ratio, 2 * cache
         dma = pltpu.SemaphoreType.DMA
         out, lse = pl.pallas_call(
@@ -370,7 +393,7 @@
             out_specs=[pl.BlockSpec(memory_space=pl.ANY)] * 2,
             scratch_shapes=[
                 pltpu.VMEM((heads, keys, hd), BF16), pltpu.VMEM((heads, hd, keys), BF16),
-                pltpu.VMEM((2, heads, NEW_PAD, hd), BF16), pltpu.VMEM((2, heads, hd, 128), BF16),
+                pltpu.VMEM((2, heads, NEW_PAD, hd), BF16), pltpu.VMEM((2, heads, hd, hd), BF16),
                 pltpu.VMEM((heads, half, 4 * tok, ratio, hd), BF16),
                 pltpu.VMEM((keys, TILE), F32), pltpu.VMEM((keys, TILE), F32),
                 pltpu.VMEM((2, NEW_PAD, TILE), F32), pltpu.VMEM((2, NEW_PAD, TILE), F32),
@@ -381,6 +404,7 @@
                 pltpu.VMEM((heads, 2 * tok, ratio, hd), BF16), pltpu.VMEM((8, rows), F32),
                 pltpu.VMEM((cache * nkv, hd), BF16), pltpu.VMEM((cache * nkv, hd), BF16), pltpu.VMEM((CHUNK * nkv, hd), F32),
                 pltpu.VMEM((heads, cache, hd), BF16), pltpu.VMEM((heads, hd, cache), BF16),
+                pltpu.VMEM((2, tok * nkv, hd), BF16), pltpu.VMEM((heads, NEW_PAD, hd), BF16), pltpu.VMEM((heads, hd, hd), BF16),
                 dma((2,)), dma((2, heads)), dma((2, heads)), dma((2, 3)),
                 dma((heads,)), dma((heads,)), dma((heads,)),
                 dma((2, heads, half)), dma((2, heads, half)),
@@ -390,7 +414,8 @@
             ],
             compiler_params=pltpu.CompilerParams(collective_id=0, has_side_effects=True, vmem_limit_bytes=60 * 2**20),
             name="ring_attend",
-        )(queries, key_cache.reshape(cache * nkv, hd), value_cache.reshape(cache * nkv, hd), kn, vn, prefix_len)
+        )(queries, key_cache.reshape(cache * nkv, hd), value_cache.reshape(cache * nkv, hd),
+          key_new.reshape(tok * nkv, hd), value_new.reshape(tok * nkv, hd), prefix_len)
         lse = lse[:, :heads].reshape(nkv, 2, tok, ratio)
         lse = lax.dynamic_index_in_dim(lse, c, axis=1, keepdims=False)
         row_lse = lse.transpose(1, 0, 2).reshape(tok, nq)

time: 127 us -> 108 us (0.85)
  Pallas kernels: 119 us -> 103 us
  local copies, waits for them, and re-layouts: 6.59 us -> 3.42 us
    pallas_call x1, Pallas kernels: 119 us -> 103 us  [local(): pl.pallas_call(functools.partial(_attend, nz, tok, heads, ratio, cache),...]
    unnamed x4 -> x2, local copies, waits for them, and re-layouts: 4.24 us -> 2.45 us
    pad x2 -> x0, local copies, waits for them, and re-layouts: 1.39 us -> none  [the longest x1 0.76 us: local(): vn = jnp.pad(value_new.transpose(1, 2, 0), ((0, 0), (0, 0), (0, 128 - tok)))]
where the time goes in v3:
time: 108 us
  Pallas kernels  103 us (95%)
  local copies, waits for them, and re-layouts  3.42 us (3%)
  between operations  1.32 us (1%)
    pallas_call x1, Pallas kernels, local(): pl.pallas_call(functools.partial(_attend, nz, tok, heads, ratio, cache),...  103 us
    unnamed x2, local copies, waits for them, and re-layouts  2.45 us

profile of v3, /device:TPU:21, one launch (start us, length us, event | category | flops | bytes accessed | tf_op | source)
XLA Modules:
  0.0 107.5 jit_solution(16802159613606668969)
XLA Ops:
  1.3 102.8 %ring_attend.1 = (bf16[24,64,128]{2,1,0:T(8,128)(2,1)}, f32[2,8,384]{2,1,0:T(8,128)}) custom-call(bf16[24,64,128]{2,1,0:T(8,128)(2,1)} %q_hbm.1, bf16[16384,128]{1,0:T(8,128)(2,1)} %bitcast.9, bf16[16384,128]{1,0:T(8,128)(2,1)} %bitcast.10, bf16[192,128]{1,0:T(8,128)(2,1)} %bitcast.12, bf16[192,128]{1,0:T(8,128)(2,1)} %bitcast.13, s32[1]{0:T(128)S(6)} %copy.11.plen_ref), custom_call_target="tpu_custom_call" | custom-call | tf_op jit(solution)/shard_map/ring_attend/pallas_call | solution.py:389
  104.1 0.7 slice.3
  104.8 0.1 reshape.26
  105.0 0.1 copy.8
  105.1 0.7 copy.9
  105.7 1.8 %copy.12 = bf16[24,64,128]{2,1,0:T(8,128)(2,1)} copy(bf16[24,64,128]{2,1,0:T(8,128)(2,1)} %get-tuple-element.10) | data formatting | bytes 786432
  (1 shorter events, 0.0 us)
